TPU v7x, 32 devices: a whole 2x2x4 slice. The times are simulated.
32 devices in a mesh: row: 4 (over y, x), col: 8 (over z, core).
Axes of the slice: x: 2, y: 2, z: 4, core: 2. Of those that a mesh axis runs over, the one named last changes fastest.
Arguments:
- trail_u: float32 [2, 4, 8, 64, 2048], P(None, 'row', 'col'), may hold values from -6 to 6
- trail_v: float32 [2, 4, 8, 64, 2048], P(None, 'row', 'col'), may hold values from -0.75 to 0.75
- ranks: int32 [2, 4, 8], P(None, 'row', 'col'), may hold values from 16 to 64
- panel_u: float32 [2, 4, 64, 2048], P(None, 'row', None, 'col'), may hold values from -6 to 6
- panel_v: float32 [2, 4, 64, 2048], P(None, 'row', None, 'col'), may hold values from -0.125 to 0.125
- locations: float32 [2, 4, 2, 2048], P(None, 'row', None, 'col'), may hold values from 0 to 1
- pend_locs: float32 [2, 2048], P(None, 'col'), may hold values from 0 to 1
- sketch: float32 [64, 2048], replicated, may hold values from -0.125 to 0.125
Outputs:
- trail_y: float32 [2, 4, 8, 64, 2048], P(None, 'row', 'col')
- trail_z: float32 [2, 4, 8, 64, 2048], P(None, 'row', 'col')
- pend_y: float32 [2, 4, 64, 2048], P(None, 'row', None, 'col')
- pend_z: float32 [2, 4, 64, 2048], P(None, 'row', None, 'col')
Inputs may be any that keep to these rules, and one draw needn't show every extreme that they name: `ranks`: ranks_ij leading columns of tile (i, j)'s left factor are in use.
All inputs are finite; a program needn't handle non-finite values.
Results may differ from a plain program's by a relative error of at most 0.0003.
Values sent between devices are 32-bit elements; how exact they have to be, the bound alone decides.
A program may use at most 64 MiB of HBM per device.

v0:
```python
import functools
import math

import jax
import jax.numpy as jnp
from jax import lax
from jax.experimental import pallas as pl
from jax.experimental.pallas import tpu as pltpu
from jax.sharding import PartitionSpec as P

matern_scale = 4.0
length_scale = 0.15
root_three = math.sqrt(3.0)
point_scale = root_three / length_scale
log2_e = math.log2(math.e)
smallest = 1e-30

MESH = pl.DeviceIdType.MESH
NN = (((1,), (0,)), ((), ()))
NT = (((1,), (1,)), ((), ()))
SLAB = 16
UNROLL = 8


def halves(value):
    high = value.astype(jnp.bfloat16)
    low = (value - high.astype(jnp.float32)).astype(jnp.bfloat16)
    return high, low


def product(left, right, dims):
    return lax.dot_general(left, right, dims, preferred_element_type=jnp.float32)


def dot3_split(left_both, right, dims):
    rows = left_both.shape[0] // 2
    right_high, right_low = halves(right)
    both = product(left_both, right_high, dims)
    return both[:rows] + both[rows:] + product(left_both[:rows], right_low, dims)


def dot3(left, right, dims):
    left_high, left_low = halves(left)
    return dot3_split(jnp.concatenate([left_high, left_low], axis=0), right, dims)


def kernel(
    n_row, n_col,
    ranks, trail_u, trail_v, panel_u, panel_v, locs, pend, sketch,
    pu_out, pj_out, acc, y_left, z_left,
    u_buf, v_buf, loc_all, pend_all, pu_all, pj_all, pv_all, g_part, g_all,
    points, own_points, sk_both, mat_high, mat_low, own_sketches,
    local_sem, loc_send, loc_recv, pend_send, pend_recv, pu_send, pu_recv,
    pj_send, pj_recv, pv_send, pv_recv, g_send, g_recv,
):
    row, col = lax.axis_index("row"), lax.axis_index("col")
    n_z = n_col // 2
    z_pos, core = col // 2, col % 2
    owner_row, owner_slot = col % n_row, col // n_row
    is_owner = row == owner_row
    slots, rank_dim, width = u_buf.shape
    w = panel_u.shape[2]
    flat = slots * rank_dim

    copy_u = pltpu.make_async_copy(trail_u, u_buf, local_sem.at[0])
    copy_v = pltpu.make_async_copy(trail_v, v_buf, local_sem.at[1])
    copy_u.start()
    copy_v.start()

    barrier = pltpu.get_barrier_semaphore()
    for step in range(1, n_col):
        pl.semaphore_signal(
            barrier, inc=1, device_id=(row, (col + step) % n_col), device_id_type=MESH)
    for step in range(1, n_row):
        pl.semaphore_signal(
            barrier, inc=1, device_id=((row + step) % n_row, col), device_id_type=MESH)

    def remote(src, dst, send, recv, to_row, to_col):
        return pltpu.make_async_remote_copy(
            src_ref=src, dst_ref=dst, send_sem=send, recv_sem=recv,
            device_id=(to_row, to_col), device_id_type=MESH)

    def loc_copy(source, step):
        return remote(locs, loc_all.at[source], loc_send.at[step], loc_recv.at[source],
                      row, (col + step) % n_col)

    def pend_copy(source, step):
        return remote(pend, pend_all.at[source], pend_send.at[step], pend_recv.at[source],
                      row, (col + step) % n_col)

    def pv_copy(source, step):
        return remote(panel_v, pv_all.at[source], pv_send.at[step], pv_recv.at[source],
                      (row + step) % n_row, col)

    def pu_copy(block, way, own=False):
        to_col = (col - 2, col + 2, 2 * z_pos + 1 - core)[way]
        src = panel_u if own else pu_all.at[block]
        return remote(src, pu_all.at[block], pu_send.at[way, block], pu_recv.at[block],
                      row, to_col)

    def pj_copy(block, step, own=False):
        src = panel_u.at[owner_slot] if own else pu_all.at[block, owner_slot]
        return remote(src, pj_all.at[block], pj_send.at[step, block], pj_recv.at[block],
                      (row + step) % n_row, col)

    def g_copy(source, step):
        target = (col + step) % n_col
        return remote(g_part.at[target], g_all.at[source], g_send.at[step], g_recv.at[source],
                      row, target)

    def to_rows(block, own=False):
        @pl.when(is_owner)
        def _():
            for step in range(1, n_row):
                pj_copy(block, step, own).start()

    sk_all = sketch[...]
    sk_high, sk_low = halves(sk_all)
    for block in range(n_col):
        sk_both[block, 0:rank_dim] = sk_high[:, block * w:(block + 1) * w]
        sk_both[block, rank_dim:2 * rank_dim] = sk_low[:, block * w:(block + 1) * w]

    pl.semaphore_wait(barrier, n_col - 1 + n_row - 1)

    for step in range(1, n_col):
        loc_copy(col, step).start()
        pend_copy(col, step).start()

    @pl.when(z_pos > 0)
    def _():
        pu_copy(col, 0, True).start()

    @pl.when(z_pos < n_z - 1)
    def _():
        pu_copy(col, 1, True).start()

    for step in range(1, n_row):
        pv_copy(row, step).start()
    pu_copy(col, 2, True).start()
    to_rows(col, True)

    pu_all[col] = panel_u[...]
    pv_all[row] = panel_v[...]
    loc_all[col] = locs[...]
    pend_all[col] = pend[...]
    acc[...] = jnp.zeros_like(acc)

    copy_u.wait()
    copy_v.wait()
    rank_iota = lax.broadcasted_iota(jnp.int32, (rank_dim, 1), 0)
    in_use = [rank_iota < ranks[slot] for slot in range(slots)]
    v_sketch = jnp.zeros((rank_dim, flat), jnp.float32)
    u_sketch = jnp.zeros((rank_dim, flat), jnp.float32)
    for block in range(n_col):
        lanes = slice(block * w, (block + 1) * w)
        sk = sk_both[block]
        v_sketch += dot3_split(sk, v_buf[:, :, lanes].reshape(flat, w), NT)
        u_block = [jnp.where(in_use[slot], u_buf[slot, :, lanes], 0.0) for slot in range(slots)]
        u_sketch += dot3_split(sk, jnp.concatenate(u_block, axis=0), NT)
    own_sketches[0] = v_sketch
    own_sketches[1] = u_sketch

    own_points[0:1, :] = jnp.concatenate(
        [locs[slot, 0:1] for slot in range(slots)] + [pend[0:1]] * slots, axis=1) * point_scale
    own_points[1:2, :] = jnp.concatenate(
        [locs[slot, 1:2] for slot in range(slots)] + [pend[1:2]] * slots, axis=1) * point_scale
    pad_rows = points.shape[2] - 2 * slots - 2

    def chunk(step):
        block = lax.rem(col + step, n_col)

        @pl.when(step > 0)
        def _():
            loc_copy(block, 1).wait_recv()
            pend_copy(block, 1).wait_recv()

        stack = [loc_all[block, slot] for slot in range(slots)] + [pend_all[block]]
        if pad_rows:
            stack.append(jnp.zeros((pad_rows, w), jnp.float32))
        points[0] = jnp.concatenate(stack, axis=0).T * point_scale

        @pl.loop(0, w // SLAB, unroll=UNROLL)
        def _(slab):
            rows = pl.ds(pl.multiple_of(slab * SLAB, SLAB), SLAB)
            at = points[0, rows, :]
            for part in range(2 * slots):
                base = 2 * slots if part < slots else 2 * (part - slots)
                lanes = slice(part * w, (part + 1) * w)
                delta_x = at[:, base:base + 1] - own_points[0:1, lanes]
                delta_y = at[:, base + 1:base + 2] - own_points[1:2, lanes]
                square = delta_x * delta_x + delta_y * delta_y
                scaled = square * lax.rsqrt(jnp.maximum(square, smallest))
                value = (1.0 + scaled) * jnp.exp2(scaled * -log2_e)
                high, low = halves(value)
                mat_high[rows, lanes] = high
                mat_low[rows, lanes] = low

        sk = sk_both[block]
        both = product(sk, mat_high[...], NN)
        acc[...] += (both[:rank_dim] + both[rank_dim:]
                     + product(sk[:rank_dim], mat_low[...], NN))

    def chunks(first, last):
        pl.loop(first, last)(chunk)

    def relay(distance):
        @pl.when(z_pos + distance < n_z)
        def _():
            block = col + 2 * distance
            pu_copy(block, 2).wait_recv()

            @pl.when(z_pos > 0)
            def _():
                pu_copy(block, 0).start()
            pu_copy(block, 2).start()
            to_rows(block)

        @pl.when(z_pos - distance >= 0)
        def _():
            block = col - 2 * distance
            pu_copy(block, 2).wait_recv()

            @pl.when(z_pos < n_z - 1)
            def _():
                pu_copy(block, 1).start()
            pu_copy(block, 2).start()
            to_rows(block)

    def from_partner(distance):
        other = 2 * z_pos + 1 - core

        @pl.when(z_pos + distance < n_z)
        def _():
            block = other + 2 * distance
            pu_copy(block, 2).wait_recv()
            to_rows(block)

        if distance:
            @pl.when(z_pos - distance >= 0)
            def _():
                block = other - 2 * distance
                pu_copy(block, 2).wait_recv()
                to_rows(block)

    def cut(piece, pieces):
        return piece * n_col // pieces

    from_partner(0)
    chunks(0, cut(1, 8))
    relay(1)
    chunks(cut(1, 8), cut(2, 8))
    for step in range(1, n_row):
        pv_copy((row + step) % n_row, 1).wait_recv()
    own_v = panel_v[...].reshape(flat, w)
    for source in range(n_row):
        for slot in range(slots):
            tile = slot * n_row + source
            if tile < n_col:
                g_part[tile] = dot3(pv_all[source, slot], own_v, NT)
    from_partner(1)
    chunks(cut(2, 8), cut(3, 8))
    for step in range(1, n_col):
        g_copy(col, step).start()
    g_all[col] = g_part[col]
    done = cut(3, 8)
    for distance in range(2, n_z):
        relay(distance)
        if distance > 2:
            from_partner(distance - 1)
        upto = min(done + cut(2, 8), n_col)
        chunks(done, upto)
        done = upto
    if n_z > 2:
        from_partner(n_z - 1)
    chunks(done, n_col)

    @pl.when(is_owner)
    def _():
        @pl.loop(0, n_col)
        def _(block):
            pj_all[block] = pu_all[block, owner_slot]

    pu_store = pltpu.make_async_copy(pu_all, pu_out, local_sem.at[0])
    pu_store.start()
    row_sketch = jnp.zeros((rank_dim, flat), jnp.float32)
    for block in range(n_col):
        row_sketch += dot3_split(sk_both[block], pu_all[block].reshape(flat, w), NT)

    for step in range(1, n_col):
        g_copy((col + step) % n_col, 1).wait_recv()
    gram = g_all[0]
    for block in range(1, n_col):
        gram = gram + g_all[block]

    @pl.when(jnp.logical_not(is_owner))
    def _():
        @pl.loop(0, n_col)
        def _(block):
            pj_copy(block, 1).wait_recv()

    pj_store = pltpu.make_async_copy(pj_all, pj_out, local_sem.at[1])
    pj_store.start()
    col_sketch = jnp.zeros((rank_dim, rank_dim), jnp.float32)
    for block in range(n_col):
        col_sketch += dot3_split(sk_both[block], pj_all[block], NT)

    left_core = dot3(col_sketch, gram, NN)
    nothing = jnp.zeros((rank_dim, 2 * rank_dim), jnp.bfloat16)

    def stacked(value):
        high, low = halves(value)
        return jnp.concatenate([
            jnp.concatenate([high, high], axis=1), jnp.concatenate([low, nothing], axis=1)
        ], axis=0)

    for slot in range(slots):
        lanes = slice(slot * rank_dim, (slot + 1) * rank_dim)
        right_core = dot3(row_sketch[:, lanes], gram[:, lanes], NT)
        y_left[slot] = stacked(
            jnp.concatenate([own_sketches[0, :, lanes], -left_core[:, lanes]], axis=1))
        z_left[slot] = stacked(
            jnp.concatenate([own_sketches[1, :, lanes], -right_core], axis=1))

    for step in range(1, n_col):
        loc_copy(col, step).wait_send()
        pend_copy(col, step).wait_send()
        g_copy(col, step).wait_send()
    for step in range(1, n_row):
        pv_copy(row, step).wait_send()
    for distance in range(n_z):
        @pl.when(z_pos + distance < n_z)
        def _(distance=distance):
            block = col + 2 * distance
            pu_copy(block, 2).wait_send()

            @pl.when(z_pos > 0)
            def _():
                pu_copy(block, 0).wait_send()

        @pl.when(z_pos - distance >= 0)
        def _(distance=distance):
            block = col - 2 * distance
            if distance:
                pu_copy(block, 2).wait_send()

            @pl.when(z_pos < n_z - 1)
            def _():
                pu_copy(block, 1).wait_send()

    @pl.when(is_owner)
    def _():
        @pl.loop(0, n_col)
        def _(block):
            for step in range(1, n_row):
                pj_copy(block, step).wait_send()

    pu_store.wait()
    pj_store.wait()


def finish(
    n_row, ranks, u_ref, v_ref, pu_ref, pj_ref, acc, y_left, z_left,
    trail_y, trail_z, pend_y, pend_z,
):
    row, col = lax.axis_index("row"), lax.axis_index("col")
    slots, rank_dim, w = u_ref.shape
    rank_iota = lax.broadcasted_iota(jnp.int32, (rank_dim, 1), 0)
    pj_high, pj_low = halves(pj_ref[0])

    def apply(left, first, second_high, second_low):
        high, low = halves(first)
        right = jnp.concatenate([high, second_high, low, second_low], axis=0)
        both = product(left, right, NN)
        return both[:rank_dim] + both[rank_dim:]

    for slot in range(slots):
        active = slot * n_row + row > col
        u_block = jnp.where(rank_iota < ranks[slot], u_ref[slot], 0.0)
        y_block = apply(y_left[slot], u_block, *halves(pu_ref[0, slot]))
        z_block = apply(z_left[slot], v_ref[slot], pj_high, pj_low)
        trail_y[slot, 0, 0] = jnp.where(active, y_block, 0.0)
        trail_z[slot, 0, 0] = jnp.where(active, z_block, 0.0)

    @pl.when(pl.program_id(0) == 0)
    def _():
        for slot in range(slots):
            lanes = slice(slot * w, (slot + 1) * w)
            pend_y[slot, 0] = acc[:, lanes] * matern_scale
            lanes = slice((slots + slot) * w, (slots + slot + 1) * w)
            pend_z[slot, 0] = acc[:, lanes] * matern_scale


def broadcast(block, axis, owner):
    block = jnp.where(lax.axis_index(axis) == owner, block, jnp.zeros_like(block))
    return lax.psum(block, axis)


def matmul(left, right):
    return jnp.dot(left, right, precision=lax.Precision.HIGHEST, preferred_element_type=jnp.float32)


def batched(form, left, right):
    return jnp.einsum(
        form, left, right, precision=lax.Precision.HIGHEST, preferred_element_type=jnp.float32
    )


def matern(row_points, col_points):
    delta_x = row_points[0][:, None] - col_points[0][None, :]
    delta_y = row_points[1][:, None] - col_points[1][None, :]
    distance = jnp.sqrt(delta_x * delta_x + delta_y * delta_y)
    scaled = root_three * distance / length_scale
    return matern_scale * (1.0 + scaled) * jnp.exp(-scaled)


def plain_on_device(trail_u, trail_v, ranks, panel_u, panel_v, locations, pend_locs, sketch):
    row_count = lax.axis_size("row")
    row_index = lax.axis_index("row")
    col_index = lax.axis_index("col")
    row_slots = trail_u.shape[0]
    rank_dim = trail_u.shape[3]
    width = trail_u.shape[4]
    local_width = pend_locs.shape[1]
    gathered_u, gathered_v = (
        lax.all_gather(panel_u, "col", axis=3, tiled=True),
        lax.all_gather(panel_v, "col", axis=3, tiled=True),
    )
    slot_index = col_index // row_count
    own_u = lax.dynamic_index_in_dim(gathered_u[:, 0], slot_index, 0, keepdims=False)
    own_v = lax.dynamic_index_in_dim(gathered_v[:, 0], slot_index, 0, keepdims=False)
    col_pu, col_pv = (
        broadcast(own_u, "row", col_index % row_count),
        broadcast(own_v, "row", col_index % row_count),
    )
    rank_iota = lax.broadcasted_iota(jnp.int32, (row_slots, rank_dim), 1)
    in_use = (rank_iota < ranks[:, 0, 0][:, None]).astype(jnp.float32)
    u_tiles = trail_u[:, 0, 0] * in_use[:, :, None]
    v_tiles = trail_v[:, 0, 0]
    row_pu = gathered_u[:, 0]
    row_pv = gathered_v[:, 0]
    v_sketch = batched("tkn,ln->tkl", v_tiles, sketch)
    u_sketch = batched("tkn,ln->tkl", u_tiles, sketch)
    cross_gram = batched("tkn,ln->tkl", row_pv, col_pv)
    col_sketch = matmul(col_pu, sketch.T)
    row_sketch = batched("tkn,ln->tkl", row_pu, sketch)
    left_core = batched("tkm,ml->tkl", cross_gram, col_sketch)
    y_tiles = batched("tkl,tkn->tln", v_sketch, u_tiles) - batched(
        "tkl,tkn->tln", left_core, row_pu
    )
    right_core = batched("tkl,tkm->tlm", row_sketch, cross_gram)
    z_tiles = batched("tkl,tkn->tln", u_sketch, v_tiles) - batched(
        "tlm,mn->tln", right_core, col_pu
    )
    tile_rows = jnp.arange(row_slots, dtype=jnp.int32) * row_count + row_index
    keep_mask = (tile_rows > col_index)[:, None, None]
    trail_y = jnp.where(keep_mask, y_tiles, 0.0).reshape(row_slots, 1, 1, rank_dim, width)
    trail_z = jnp.where(keep_mask, z_tiles, 0.0).reshape(row_slots, 1, 1, rank_dim, width)
    y_list = []
    z_list = []
    rows_all, pend_all = (
        lax.all_gather(locations, "col", axis=3, tiled=True),
        lax.all_gather(pend_locs.reshape(1, 1, 2, local_width), "col", axis=3, tiled=True),
    )
    col_points = pend_all[0, 0]
    for slot_num in range(row_slots):
        own_kernel = matern(locations[slot_num, 0], col_points)
        y_list.append(matmul(sketch, own_kernel.T))
        col_kernel = matern(rows_all[slot_num, 0], pend_locs)
        z_list.append(matmul(sketch, col_kernel))
    pend_y = jnp.stack(y_list)
    pend_z = jnp.stack(z_list)
    pend_y = pend_y.reshape(row_slots, 1, rank_dim, local_width)
    pend_z = pend_z.reshape(row_slots, 1, rank_dim, local_width)
    return (trail_y, trail_z, pend_y, pend_z)


def on_device(n_row, n_col, trail_u, trail_v, ranks, panel_u, panel_v, locations, pend_locs, sketch):
    slots, _, _, rank_dim, width = trail_u.shape
    w = pend_locs.shape[1]
    if w % 128 or rank_dim % 16 or n_col % 2:
        return plain_on_device(
            trail_u, trail_v, ranks, panel_u, panel_v, locations, pend_locs, sketch
        )
    flat = slots * rank_dim
    f32, bf16 = jnp.float32, jnp.bfloat16
    dma = pltpu.SemaphoreType.DMA
    vmem = pl.BlockSpec(memory_space=pltpu.VMEM)
    hbm = pl.BlockSpec(memory_space=pl.ANY)
    point_rows = -(-(2 * slots + 2) // 8) * 8
    ranks = ranks.reshape(slots)
    trail_u = trail_u.reshape(slots, rank_dim, width)
    trail_v = trail_v.reshape(slots, rank_dim, width)
    shape = jax.ShapeDtypeStruct
    smem = pl.BlockSpec(memory_space=pltpu.SMEM)
    pu_all, pj_all, acc, y_left, z_left = pl.pallas_call(
        functools.partial(kernel, n_row, n_col),
        out_shape=(
            shape((n_col, slots, rank_dim, w), f32),
            shape((n_col, rank_dim, w), f32),
            shape((rank_dim, 2 * slots * w), f32),
            shape((slots, 2 * rank_dim, 4 * rank_dim), bf16),
            shape((slots, 2 * rank_dim, 4 * rank_dim), bf16),
        ),
        in_specs=[smem, hbm, hbm] + [vmem] * 5,
        out_specs=(hbm, hbm, vmem, vmem, vmem),
        scratch_shapes=[
            pltpu.VMEM((slots, rank_dim, width), f32),
            pltpu.VMEM((slots, rank_dim, width), f32),
            pltpu.VMEM((n_col, slots, 2, w), f32),
            pltpu.VMEM((n_col, 2, w), f32),
            pltpu.VMEM((n_col, slots, rank_dim, w), f32),
            pltpu.VMEM((n_col, rank_dim, w), f32),
            pltpu.VMEM((n_row, slots, rank_dim, w), f32),
            pltpu.VMEM((n_col, rank_dim, flat), f32),
            pltpu.VMEM((n_col, rank_dim, flat), f32),
            pltpu.VMEM((1, w, point_rows), f32),
            pltpu.VMEM((2, 2 * slots * w), f32),
            pltpu.VMEM((n_col, 2 * rank_dim, w), bf16),
            pltpu.VMEM((w, 2 * slots * w), bf16),
            pltpu.VMEM((w, 2 * slots * w), bf16),
            pltpu.VMEM((2, rank_dim, flat), f32),
            dma((2,)),
            dma((n_col,)), dma((n_col,)), dma((n_col,)), dma((n_col,)),
            dma((3, n_col)), dma((n_col,)),
            dma((n_row, n_col)), dma((n_col,)),
            dma((n_row,)), dma((n_row,)),
            dma((n_col,)), dma((n_col,)),
        ],
        compiler_params=pltpu.CompilerParams(collective_id=0, has_side_effects=True),
    )(
        ranks,
        trail_u,
        trail_v,
        panel_u.reshape(slots, rank_dim, w),
        panel_v.reshape(slots, rank_dim, w),
        locations.reshape(slots, 2, w),
        pend_locs,
        sketch,
    )
    tile = pl.BlockSpec((slots, rank_dim, w), lambda block: (0, 0, block))
    out_tile = pl.BlockSpec((slots, 1, 1, rank_dim, w), lambda block: (0, 0, 0, 0, block))
    left = pl.BlockSpec((slots, 2 * rank_dim, 4 * rank_dim), lambda block: (0, 0, 0))
    pend_tile = pl.BlockSpec((slots, 1, rank_dim, w), lambda block: (0, 0, 0, 0))
    return pl.pallas_call(
        functools.partial(finish, n_row),
        grid=(n_col,),
        out_shape=(
            shape((slots, 1, 1, rank_dim, width), f32),
            shape((slots, 1, 1, rank_dim, width), f32),
            shape((slots, 1, rank_dim, w), f32),
            shape((slots, 1, rank_dim, w), f32),
        ),
        in_specs=[
            smem, tile, tile,
            pl.BlockSpec((1, slots, rank_dim, w), lambda block: (block, 0, 0, 0)),
            pl.BlockSpec((1, rank_dim, w), lambda block: (block, 0, 0)),
            pl.BlockSpec((rank_dim, 2 * slots * w), lambda block: (0, 0)),
            left, left,
        ],
        out_specs=(out_tile, out_tile, pend_tile, pend_tile),
    )(ranks, trail_u, trail_v, pu_all, pj_all, acc, y_left, z_left)


def solution(mesh):
    in_specs = (
        P(None, "row", "col", None, None),
        P(None, "row", "col", None, None),
        P(None, "row", "col"),
        P(None, "row", None, "col"),
        P(None, "row", None, "col"),
        P(None, "row", None, "col"),
        P(None, "col"),
        P(),
    )
    out_specs = (
        P(None, "row", "col", None, None),
        P(None, "row", "col", None, None),
        P(None, "row", None, "col"),
        P(None, "row", None, "col"),
    )
    body = functools.partial(on_device, mesh.shape["row"], mesh.shape["col"])
    return jax.shard_map(
        body, mesh=mesh, in_specs=in_specs, out_specs=out_specs, check_vma=False
    )
```

profile of v0, /device:TPU:6, one launch (start us, length us, event | category | flops | bytes accessed | tf_op | source)
XLA Modules:
  0.0 39.7 jit_solution(10594651486483686751)
XLA Ops:
  0.6 31.8 %shard_map.111 = (f32[8,2,64,256]{3,2,1,0:T(8,128)}, f32[8,64,256]{2,1,0:T(8,128)}, f32[64,1024]{1,0:T(8,128)}, bf16[2,128,256]{2,1,0:T(8,128)(2,1)}, bf16[2,128,256]{2,1,0:T(8,128)(2,1)}) custom-call(s32[2]{0:T(128)} %bitcast.13, f32[2,64,2048]{2,1,0:T(8,128)} %bitcast.6, f32[2,64,2048]{2,1,0:T(8,128)} %bitcast.8, f32[2,64,256]{2,1,0:T(8,128)} %bitcast.10, ...), custom_call_target="tpu_custom_call" | custom-call | tf_op jit(solution)/shard_map/pallas_call | solution.py:495
  32.4 7.2 %shard_map.112 = (f32[2,1,1,64,2048]{4,3,2,1,0:T(8,128)}, f32[2,1,1,64,2048]{4,3,2,1,0:T(8,128)}, f32[2,1,64,256]{3,2,1,0:T(8,128)}, f32[2,1,64,256]{3,2,1,0:T(8,128)}) custom-call(s32[2]{0:T(128)} %bitcast.14, f32[2,64,2048]{2,1,0:T(8,128)} %bitcast.7, f32[2,64,2048]{2,1,0:T(8,128)} %bitcast.9, f32[8,2,64,256]{3,2,1,0:T(8,128)} %get-tuple-element.9.pu_ref, ...), custom_call_target="tpu_custom_call" | custom-call | tf_op jit(solution)/shard_map/pallas_call | solution.py:544
where the time goes:
time: 40.3 us; the launch traced here: 39.7 us
  Pallas kernels  39 us (97%)
  between operations  0.64 us (2%)
    pallas_call x1, Pallas kernels, on_device(): pl.pallas_call(functools.partial(kernel, n_row, n_col), out_shape=(shape(...  31.8 us
    pallas_call x1, Pallas kernels, on_device(): pl.pallas_call(functools.partial(finish, n_row), grid=(n_col,), out_shape...  7.24 us

commit v1 on v0

v1 whole, which is shorter than its diff:
```python
import functools
import math

import jax
import jax.numpy as jnp
from jax import lax
from jax.experimental import pallas as pl
from jax.experimental.pallas import tpu as pltpu
from jax.sharding import PartitionSpec as P

matern_scale = 4.0
length_scale = 0.15
root_three = math.sqrt(3.0)
point_scale = root_three / length_scale
log2_e = math.log2(math.e)
smallest = 1e-30

MESH = pl.DeviceIdType.MESH
NN = (((1,), (0,)), ((), ()))
NT = (((1,), (1,)), ((), ()))
SLAB = 16
UNROLL = 8
VMEM_LIMIT = 32 << 20


def halves(value):
    high = value.astype(jnp.bfloat16)
    low = (value - high.astype(jnp.float32)).astype(jnp.bfloat16)
    return high, low


def product(left, right, dims):
    return lax.dot_general(left, right, dims, preferred_element_type=jnp.float32)


def dot3_split(left_both, right, dims):
    rows = left_both.shape[0] // 2
    right_high, right_low = halves(right)
    both = product(left_both, right_high, dims)
    return both[:rows] + both[rows:] + product(left_both[:rows], right_low, dims)


def dot3(left, right, dims):
    left_high, left_low = halves(left)
    return dot3_split(jnp.concatenate([left_high, left_low], axis=0), right, dims)


def kernel(
    n_row, n_col,
    ranks, trail_u, trail_v, panel_u, panel_v, locs, pend, sketch,
    ru, rv, rp, rj, y_left, z_left, pend_acc,
    u_buf, v_buf, sk_buf, loc_all, pu_all, pj_all, pv_all, g_part, g_peer, g_sum, g_all,
    points, own_points, sk_both, mat_high, mat_low, acc, own_sketches, row_sketch, col_sketch,
    far_sem, load_sem, trail_sem, loc_send, loc_recv, pu_send, pf_send, pr_send, pu_recv,
    pv_send, pv_recv, pj_send, pj_recv, gx_send, gx_recv, g_send, g_recv,
):
    row, col = lax.axis_index("row"), lax.axis_index("col")
    n_z = n_col // 2
    z, core = col // 2, col % 2
    other = 1 - core
    partner = 2 * z + other
    slots, rank_dim, width = u_buf.shape
    w = pu_all.shape[3]
    half_z = n_row // 2
    last = (slots - 1) * n_row
    owner_row, owner_slot = col % n_row, col // n_row
    is_owner = row == owner_row
    x_row = row + 1 - 2 * (row % 2)
    y_row = (row + half_z) % n_row
    any_active = last + row > col

    def active(slot):
        return slot * n_row + row > col

    def needs(slot, chip):
        return 2 * chip <= slot * n_row + row

    def carries(slot, chip, source):
        return jnp.logical_or(
            needs(slot, chip), jnp.logical_and(chip == 1, source >= 2))

    def direct(slot, chip, source):
        return jnp.logical_and(
            carries(slot, chip, source),
            jnp.logical_or(chip > 0, source < 2))

    def chip_at(step):
        over = (z + step) // n_z
        return z + step + over * (n_z - 1 - 2 * step - z)

    def wants_column(at_row):
        return last + at_row > col

    def remote(src, dst, send, recv, to_row, to_col):
        return pltpu.make_async_remote_copy(
            src_ref=src, dst_ref=dst, send_sem=send, recv_sem=recv,
            device_id=(to_row, to_col), device_id_type=MESH)

    def loc_copy(source, target):
        return remote(loc_all.at[source], loc_all.at[source], loc_send.at[target],
                      loc_recv.at[source], row, target)

    def pv_copy(slot, source, target):
        return remote(pv_all.at[source, slot], pv_all.at[source, slot],
                      pv_send.at[slot, target], pv_recv.at[slot, source], target, col)

    def pu_copy(slot, block, send, target):
        return remote(pu_all.at[block, slot], pu_all.at[block, slot], send,
                      pu_recv.at[slot, block], row, target)

    def pu_direct(slot, chip):
        return pu_copy(slot, col, pu_send.at[slot, chip], 2 * chip + core)

    def pu_partner(slot, block):
        return pu_copy(slot, block, pf_send.at[slot, block], partner)

    def pu_relay(slot, block):
        return pu_copy(slot, block, pr_send.at[slot, block], core)

    def pj_copy(block, way):
        src = pj_all.at[block] if way == 2 else pu_all.at[block, owner_slot]
        return remote(src, pj_all.at[block], pj_send.at[way, block], pj_recv.at[block],
                      y_row if way == 1 else x_row, col)

    def gx_copy(batch):
        chips = pl.ds(batch * half_z, half_z)
        return remote(g_part.at[other, chips], g_peer.at[chips], gx_send.at[batch],
                      gx_recv.at[batch], row, partner)

    def g_copy(source, chip):
        return remote(g_sum.at[chip], g_all.at[source], g_send.at[chip], g_recv.at[source],
                      row, 2 * chip + core)

    def when(*terms):
        return pl.when(functools.reduce(jnp.logical_and, terms))

    to_y = jnp.logical_or(wants_column(y_row), wants_column(n_row - 1 - row))
    y_of_owner = row == (owner_row + half_z) % n_row
    is_relay = jnp.logical_and(y_of_owner, wants_column(x_row))
    takes_column = jnp.logical_and(
        jnp.logical_not(is_owner),
        jnp.logical_or(wants_column(row), is_relay))

    barrier = pltpu.get_barrier_semaphore()

    def hello(semaphore, to_row, to_col):
        pl.semaphore_signal(semaphore, inc=1, device_id=(to_row, to_col), device_id_type=MESH)

    for step in range(1, n_row):
        hello(barrier, (row + step) % n_row, col)
    hello(barrier, row, partner)
    for chip in range(1, n_z):
        @pl.when(z < chip)
        def _(chip=chip):
            hello(barrier, row, 2 * chip)
            hello(barrier, row, 2 * chip + 1)

    loads = [
        pltpu.make_async_copy(locs, loc_all.at[col, pl.ds(0, slots)], load_sem.at[0]),
        pltpu.make_async_copy(pend, loc_all.at[col, slots], load_sem.at[1]),
        pltpu.make_async_copy(panel_v, pv_all.at[row], load_sem.at[2]),
        pltpu.make_async_copy(panel_u, pu_all.at[col], load_sem.at[3]),
        pltpu.make_async_copy(sketch, sk_buf, load_sem.at[4]),
    ]
    for load in loads:
        load.start()

    def trail_load(slot, which):
        src, dst = ((trail_u, u_buf), (trail_v, v_buf))[which]
        return pltpu.make_async_copy(src.at[slot], dst.at[slot], trail_sem.at[slot, which])

    for slot in range(slots):
        @pl.when(active(slot))
        def _(slot=slot):
            trail_load(slot, 0).start()
            trail_load(slot, 1).start()

    for load in loads[:4]:
        load.wait()
    pl.semaphore_wait(barrier, n_row + 2 * z)

    for chip in range(n_z - 1):
        @pl.when(z > chip)
        def _(chip=chip):
            hello(far_sem, row, 2 * chip)
            hello(far_sem, row, 2 * chip + 1)

    def each_loc(act, higher):
        for chip in range(n_z):
            @pl.when(z < chip if higher else z > chip)
            def _(chip=chip):
                act(loc_copy(col, 2 * chip))
                act(loc_copy(col, 2 * chip + 1))

    def each_direct(act, higher, slot):
        for chip in (range(1, n_z) if higher else reversed(range(n_z - 1))):
            @when(z < chip if higher else z > chip, direct(slot, chip, z))
            def _(chip=chip):
                act(pu_direct(slot, chip))

    def each_pv(act, slot):
        for step in range(1, n_row):
            target = (row + step) % n_row

            @pl.when(last + target > slot * n_row + row)
            def _(target=target):
                act(pv_copy(slot, row, target))

    def each_column(act, block, slot=None):
        ours = is_owner if slot is None else jnp.logical_and(is_owner, owner_slot == slot)

        @when(ours, wants_column(x_row))
        def _():
            act(pj_copy(block, 0))

        @when(ours, to_y)
        def _():
            act(pj_copy(block, 1))

    def start(copy):
        copy.start()

    def wait_send(copy):
        copy.wait_send()

    start(loc_copy(col, partner))
    each_loc(start, False)
    each_pv(start, 0)
    for slot in range(slots):
        each_direct(start, False, slot)

        @pl.when(needs(slot, z))
        def _(slot=slot):
            start(pu_partner(slot, col))
    each_column(start, col)
    for slot in range(1, slots):
        each_pv(start, slot)

    loads[4].wait()
    sk_high, sk_low = halves(sk_buf[...])
    for block in range(n_col):
        sk_both[block, 0:rank_dim] = sk_high[:, block * w:(block + 1) * w]
        sk_both[block, rank_dim:2 * rank_dim] = sk_low[:, block * w:(block + 1) * w]

    acc[...] = jnp.zeros_like(acc)
    row_sketch[...] = jnp.zeros_like(row_sketch)
    col_sketch[...] = jnp.zeros_like(col_sketch)
    own_points[0:1, :] = jnp.concatenate(
        [loc_all[col, slot, 0:1] for slot in range(slots)] + [loc_all[col, slots, 0:1]] * slots,
        axis=1) * point_scale
    own_points[1:2, :] = jnp.concatenate(
        [loc_all[col, slot, 1:2] for slot in range(slots)] + [loc_all[col, slots, 1:2]] * slots,
        axis=1) * point_scale
    pad_rows = points.shape[2] - 2 * slots - 2

    def chunk(step):
        block = 2 * chip_at(step // 2) + (core + step) % 2

        @pl.when(step > 0)
        def _():
            loc_copy(block, partner).wait_recv()

        stack = [loc_all[block, slot] for slot in range(slots + 1)]
        if pad_rows:
            stack.append(jnp.zeros((pad_rows, w), jnp.float32))
        points[0] = jnp.concatenate(stack, axis=0).T * point_scale

        @pl.loop(0, w // SLAB, unroll=UNROLL)
        def _(slab):
            rows = pl.ds(pl.multiple_of(slab * SLAB, SLAB), SLAB)
            at = points[0, rows, :]
            for part in range(2 * slots):
                base = 2 * slots if part < slots else 2 * (part - slots)
                lanes = slice(part * w, (part + 1) * w)
                delta_x = at[:, base:base + 1] - own_points[0:1, lanes]
                delta_y = at[:, base + 1:base + 2] - own_points[1:2, lanes]
                square = delta_x * delta_x + delta_y * delta_y
                scaled = square * lax.rsqrt(jnp.maximum(square, smallest))
                value = (1.0 + scaled) * jnp.exp2(scaled * -log2_e)
                high, low = halves(value)
                mat_high[rows, lanes] = high
                mat_low[rows, lanes] = low

        sk = sk_both[block]
        both = product(sk, mat_high[...], NN)
        acc[...] += (both[:rank_dim] + both[rank_dim:]
                     + product(sk[:rank_dim], mat_low[...], NN))

    def chunks(first, final):
        pl.loop(first * n_col // 8, final * n_col // 8)(chunk)

    def sketch_of(block, high, low):
        sk = sk_both[block]
        both = product(sk, high, NT)
        return both[:rank_dim] + both[rank_dim:] + product(sk[:rank_dim], low, NT)

    def own_sketch(slot):
        trail_load(slot, 0).wait()
        trail_load(slot, 1).wait()
        in_use = lax.broadcasted_iota(jnp.int32, (rank_dim, 1), 0) < ranks[slot]
        v_sketch = jnp.zeros((rank_dim, rank_dim), jnp.float32)
        u_sketch = jnp.zeros((rank_dim, rank_dim), jnp.float32)
        for block in range(n_col):
            lanes = slice(block * w, (block + 1) * w)
            high, low = halves(v_buf[slot, :, lanes])
            rv[slot, 0, :, lanes] = high
            rv[slot, 1, :, lanes] = low
            v_sketch += sketch_of(block, high, low)
            high, low = halves(jnp.where(in_use, u_buf[slot, :, lanes], 0.0))
            ru[slot, 0, :, lanes] = high
            ru[slot, 1, :, lanes] = low
            u_sketch += sketch_of(block, high, low)
        own_sketches[slot, 0] = v_sketch
        own_sketches[slot, 1] = u_sketch

    def own_all():
        for slot in range(slots):
            @pl.when(active(slot))
            def _(slot=slot):
                own_sketch(slot)

    def arrive(slot, step):
        chip = chip_at(step)
        block = 2 * chip + core

        @pl.when(carries(slot, z, chip))
        def _():
            pu_partner(slot, block).wait_recv()

            @when(z == 1, chip >= 2)
            def _():
                pu_relay(slot, block).start()

            @pl.when(needs(slot, z))
            def _():
                pu_partner(slot, block).start()
            each_column(start, block, slot)

    def from_partner(slot, step):
        block = 2 * chip_at(step) + other

        @pl.when(needs(slot, z))
        def _():
            pu_partner(slot, block).wait_recv()
            each_column(start, block, slot)

    def column(step):
        for flip in range(2):
            block = 2 * chip_at(step) + (core + flip) % 2

            @pl.when(takes_column)
            def _():
                pj_copy(block, 0).wait_recv()

                @pl.when(is_relay)
                def _():
                    pj_copy(block, 2).start()

    def gram_part(slot):
        own_v = pv_all[row].reshape(slots * rank_dim, w)
        own_high, own_low = halves(own_v)
        for source in range(n_row):
            tile = slot * n_row + source

            @pl.when(last + row > tile)
            def _(source=source, tile=tile):
                @pl.when(row != source)
                def _():
                    pv_copy(slot, source, row).wait_recv()
                high, low = halves(pv_all[source, slot])
                both = product(jnp.concatenate([high, low], axis=0), own_high, NT)
                g_part[tile % 2, tile // 2] = (
                    both[:rank_dim] + both[rank_dim:] + product(high, own_low, NT))

    def has_batch(batch):
        return last + row > batch * n_row

    def gram_swap(batch):
        @pl.when(has_batch(batch))
        def _():
            gx_copy(batch).start()

    def gram_sum(batch):
        @pl.when(has_batch(batch))
        def _():
            gx_copy(batch).wait_recv()
            for chip in range(batch * half_z, (batch + 1) * half_z):
                g_sum[chip] = g_part[core, chip] + g_peer[chip]

    def each_gram(act, batch):
        for chip in range(batch * half_z, (batch + 1) * half_z):
            @when(last + row > 2 * chip + core, z != chip)
            def _(chip=chip):
                act(g_copy(z, chip))

    def blocks_of(first, final):
        return [2 * chip_at(step) + flip for step in range(first, final) for flip in range(2)]

    def absorb_rows(slot, first, final):
        @pl.when(active(slot))
        def _():
            total = row_sketch[slot]
            for block in blocks_of(first, final):
                lanes = pl.ds(pl.multiple_of(block * w, w), w)
                high, low = halves(pu_all[block, slot])
                rp[slot, 0, :, lanes] = high
                rp[slot, 1, :, lanes] = low
                total += sketch_of(block, high, low)
            row_sketch[slot] = total

    def absorb_column(first, final):
        @pl.when(any_active)
        def _():
            @pl.when(is_owner)
            def _():
                for block in blocks_of(first, final):
                    pj_all[block] = pu_all[block, owner_slot]
            total = col_sketch[...]
            for block in blocks_of(first, final):
                lanes = pl.ds(pl.multiple_of(block * w, w), w)
                high, low = halves(pj_all[block])
                rj[0, :, lanes] = high
                rj[1, :, lanes] = low
                total += sketch_of(block, high, low)
            col_sketch[...] = total

    def upward():
        @pl.when(z < n_z - 1)
        def _():
            pl.semaphore_wait(far_sem, 2 * (n_z - 1 - z))
        each_loc(start, True)
        for slot in range(slots):
            each_direct(start, True, slot)

    chunks(0, 2)
    own_all()
    upward()
    for slot in range(slots):
        from_partner(slot, 0)
    gram_part(0)
    for slot in range(slots):
        arrive(slot, 1)
    column(0)
    gram_swap(0)
    chunks(2, 3)
    gram_sum(0)
    for slot in range(slots):
        from_partner(slot, 1)
    arrive(0, 2)
    each_gram(start, 0)
    chunks(3, 4)
    for slot in range(1, slots):
        arrive(slot, 2)
    column(1)
    for slot in range(1, slots):
        gram_part(slot)
    from_partner(0, 2)
    chunks(4, 5)
    for slot in range(1, slots):
        gram_swap(slot)
    for slot in range(1, slots):
        from_partner(slot, 2)
    arrive(0, 3)
    column(2)
    chunks(5, 6)
    for slot in range(1, slots):
        gram_sum(slot)
    for slot in range(1, slots):
        arrive(slot, 3)
    from_partner(0, 3)
    for slot in range(slots):
        absorb_rows(slot, 0, n_z - 1)
    for slot in range(1, slots):
        each_gram(start, slot)
    absorb_column(0, n_z - 1)
    chunks(6, 8)
    pend_acc[...] = acc[...] * matern_scale
    column(3)
    for slot in range(1, slots):
        from_partner(slot, 3)
    for slot in range(slots):
        absorb_rows(slot, n_z - 1, n_z)
    absorb_column(n_z - 1, n_z)

    @pl.when(any_active)
    def _():
        gram = g_sum[z]
        for step in range(1, n_z):
            chip = chip_at(step)
            g_copy(chip, z).wait_recv()
            gram = gram + g_all[chip]
        left_core = dot3(col_sketch[...], gram, NN)
        nothing = jnp.zeros((rank_dim, 2 * rank_dim), jnp.bfloat16)

        def stacked(value):
            high, low = halves(value)
            return jnp.concatenate([
                jnp.concatenate([high, high], axis=1), jnp.concatenate([low, nothing], axis=1)
            ], axis=0)

        for slot in range(slots):
            lanes = slice(slot * rank_dim, (slot + 1) * rank_dim)

            @pl.when(active(slot))
            def _(slot=slot, lanes=lanes):
                right_core = dot3(row_sketch[slot], gram[:, lanes], NT)
                y_left[slot] = stacked(
                    jnp.concatenate([own_sketches[slot, 0], -left_core[:, lanes]], axis=1))
                z_left[slot] = stacked(
                    jnp.concatenate([own_sketches[slot, 1], -right_core], axis=1))

    wait_send(loc_copy(col, partner))
    for higher in (False, True):
        each_loc(wait_send, higher)
        for slot in range(slots):
            each_direct(wait_send, higher, slot)
    for slot in range(slots):
        each_pv(wait_send, slot)
        each_gram(wait_send, slot)

        @pl.when(has_batch(slot))
        def _(slot=slot):
            gx_copy(slot).wait_send()
        for step in range(n_z):
            chip = chip_at(step)
            block = 2 * chip + core

            @pl.when(needs(slot, z))
            def _(slot=slot, block=block):
                pu_partner(slot, block).wait_send()

            @when(z == 1, chip >= 2)
            def _(slot=slot, block=block):
                pu_relay(slot, block).wait_send()

    @pl.loop(0, n_col)
    def _(block):
        each_column(wait_send, block)

        @pl.when(is_relay)
        def _():
            pj_copy(block, 2).wait_send()


def finish(
    n_row, ru, rv, rp, rj, y_left, z_left, pend_acc,
    trail_y, trail_z, pend_y, pend_z,
    y_buf, z_buf, out_sem, pend_sem,
):
    row, col = lax.axis_index("row"), lax.axis_index("col")
    slots, _, rank_dim, width = ru.shape
    w = pend_y.shape[3]
    pieces = out_sem.shape[2]
    span = width // pieces

    def pend_copy(slot, which):
        lanes = pl.ds((which * slots + slot) * w, w)
        return pltpu.make_async_copy(
            pend_acc.at[:, lanes], (pend_y, pend_z)[which].at[slot, 0], pend_sem.at[slot, which])

    def out_copy(slot, which, piece):
        lanes = pl.ds(piece * span, span)
        src, dst = ((y_buf, trail_y), (z_buf, trail_z))[which]
        return pltpu.make_async_copy(
            src.at[slot, :, lanes], dst.at[slot, 0, 0, :, lanes], out_sem.at[slot, which, piece])

    for slot in range(slots):
        pend_copy(slot, 0).start()
        pend_copy(slot, 1).start()

    for slot in range(slots):
        active = slot * n_row + row > col

        @pl.when(jnp.logical_not(active))
        def _(slot=slot):
            y_buf[slot] = jnp.zeros((rank_dim, width), jnp.float32)
            z_buf[slot] = jnp.zeros((rank_dim, width), jnp.float32)
            for which in range(2):
                for piece in range(pieces):
                    out_copy(slot, which, piece).start()

        @pl.when(active)
        def _(slot=slot):
            for which in range(2):
                left = (y_left, z_left)[which][slot]
                first = (ru, rv)[which]
                buf = (y_buf, z_buf)[which]
                for piece in range(pieces):
                    lanes = slice(piece * span, (piece + 1) * span)
                    second = [rj[part, :, lanes] if which else rp[slot, part, :, lanes]
                              for part in range(2)]
                    right = jnp.concatenate(
                        [first[slot, 0, :, lanes], second[0], first[slot, 1, :, lanes], second[1]],
                        axis=0)
                    both = product(left, right, NN)
                    buf[slot, :, lanes] = both[:rank_dim] + both[rank_dim:]
                    out_copy(slot, which, piece).start()

    for slot in range(slots):
        for which in range(2):
            pend_copy(slot, which).wait()
            for piece in range(pieces):
                out_copy(slot, which, piece).wait()


def broadcast(block, axis, owner):
    block = jnp.where(lax.axis_index(axis) == owner, block, jnp.zeros_like(block))
    return lax.psum(block, axis)


def matmul(left, right):
    return jnp.dot(left, right, precision=lax.Precision.HIGHEST, preferred_element_type=jnp.float32)


def batched(form, left, right):
    return jnp.einsum(
        form, left, right, precision=lax.Precision.HIGHEST, preferred_element_type=jnp.float32
    )


def matern(row_points, col_points):
    delta_x = row_points[0][:, None] - col_points[0][None, :]
    delta_y = row_points[1][:, None] - col_points[1][None, :]
    distance = jnp.sqrt(delta_x * delta_x + delta_y * delta_y)
    scaled = root_three * distance / length_scale
    return matern_scale * (1.0 + scaled) * jnp.exp(-scaled)


def plain_on_device(trail_u, trail_v, ranks, panel_u, panel_v, locations, pend_locs, sketch):
    row_count = lax.axis_size("row")
    row_index = lax.axis_index("row")
    col_index = lax.axis_index("col")
    row_slots = trail_u.shape[0]
    rank_dim = trail_u.shape[3]
    width = trail_u.shape[4]
    local_width = pend_locs.shape[1]
    gathered_u, gathered_v = (
        lax.all_gather(panel_u, "col", axis=3, tiled=True),
        lax.all_gather(panel_v, "col", axis=3, tiled=True),
    )
    slot_index = col_index // row_count
    own_u = lax.dynamic_index_in_dim(gathered_u[:, 0], slot_index, 0, keepdims=False)
    own_v = lax.dynamic_index_in_dim(gathered_v[:, 0], slot_index, 0, keepdims=False)
    col_pu, col_pv = (
        broadcast(own_u, "row", col_index % row_count),
        broadcast(own_v, "row", col_index % row_count),
    )
    rank_iota = lax.broadcasted_iota(jnp.int32, (row_slots, rank_dim), 1)
    in_use = (rank_iota < ranks[:, 0, 0][:, None]).astype(jnp.float32)
    u_tiles = trail_u[:, 0, 0] * in_use[:, :, None]
    v_tiles = trail_v[:, 0, 0]
    row_pu = gathered_u[:, 0]
    row_pv = gathered_v[:, 0]
    v_sketch = batched("tkn,ln->tkl", v_tiles, sketch)
    u_sketch = batched("tkn,ln->tkl", u_tiles, sketch)
    cross_gram = batched("tkn,ln->tkl", row_pv, col_pv)
    col_sketch = matmul(col_pu, sketch.T)
    row_sketch = batched("tkn,ln->tkl", row_pu, sketch)
    left_core = batched("tkm,ml->tkl", cross_gram, col_sketch)
    y_tiles = batched("tkl,tkn->tln", v_sketch, u_tiles) - batched(
        "tkl,tkn->tln", left_core, row_pu
    )
    right_core = batched("tkl,tkm->tlm", row_sketch, cross_gram)
    z_tiles = batched("tkl,tkn->tln", u_sketch, v_tiles) - batched(
        "tlm,mn->tln", right_core, col_pu
    )
    tile_rows = jnp.arange(row_slots, dtype=jnp.int32) * row_count + row_index
    keep_mask = (tile_rows > col_index)[:, None, None]
    trail_y = jnp.where(keep_mask, y_tiles, 0.0).reshape(row_slots, 1, 1, rank_dim, width)
    trail_z = jnp.where(keep_mask, z_tiles, 0.0).reshape(row_slots, 1, 1, rank_dim, width)
    y_list = []
    z_list = []
    rows_all, pend_all = (
        lax.all_gather(locations, "col", axis=3, tiled=True),
        lax.all_gather(pend_locs.reshape(1, 1, 2, local_width), "col", axis=3, tiled=True),
    )
    col_points = pend_all[0, 0]
    for slot_num in range(row_slots):
        own_kernel = matern(locations[slot_num, 0], col_points)
        y_list.append(matmul(sketch, own_kernel.T))
        col_kernel = matern(rows_all[slot_num, 0], pend_locs)
        z_list.append(matmul(sketch, col_kernel))
    pend_y = jnp.stack(y_list)
    pend_z = jnp.stack(z_list)
    pend_y = pend_y.reshape(row_slots, 1, rank_dim, local_width)
    pend_z = pend_z.reshape(row_slots, 1, rank_dim, local_width)
    return (trail_y, trail_z, pend_y, pend_z)


def on_device(n_row, n_col, trail_u, trail_v, ranks, panel_u, panel_v, locations, pend_locs, sketch):
    slots, _, _, rank_dim, width = trail_u.shape
    w = pend_locs.shape[1]
    n_z = n_col // 2
    fits = n_col == slots * n_row and n_row == 4 and slots == 2
    if w % 128 or rank_dim % 16 or not fits:
        return plain_on_device(
            trail_u, trail_v, ranks, panel_u, panel_v, locations, pend_locs, sketch
        )
    flat = slots * rank_dim
    f32, bf16 = jnp.float32, jnp.bfloat16
    dma = pltpu.SemaphoreType.DMA
    vmem = pl.BlockSpec(memory_space=pltpu.VMEM)
    hbm = pl.BlockSpec(memory_space=pltpu.HBM)
    smem = pl.BlockSpec(memory_space=pltpu.SMEM)
    point_rows = -(-(2 * slots + 2) // 8) * 8
    shape = jax.ShapeDtypeStruct
    kept = pl.pallas_call(
        functools.partial(kernel, n_row, n_col),
        out_shape=(
            pltpu.VMEM((slots, 2, rank_dim, width), bf16),
            pltpu.VMEM((slots, 2, rank_dim, width), bf16),
            pltpu.VMEM((slots, 2, rank_dim, width), bf16),
            pltpu.VMEM((2, rank_dim, width), bf16),
            pltpu.VMEM((slots, 2 * rank_dim, 4 * rank_dim), bf16),
            pltpu.VMEM((slots, 2 * rank_dim, 4 * rank_dim), bf16),
            pltpu.VMEM((rank_dim, 2 * slots * w), f32),
        ),
        in_specs=[smem] + [hbm] * 7,
        out_specs=(vmem,) * 7,
        scratch_shapes=[
            pltpu.VMEM((slots, rank_dim, width), f32),
            pltpu.VMEM((slots, rank_dim, width), f32),
            pltpu.VMEM((rank_dim, width), f32),
            pltpu.VMEM((n_col, slots + 1, 2, w), f32),
            pltpu.VMEM((n_col, slots, rank_dim, w), f32),
            pltpu.VMEM((n_col, rank_dim, w), f32),
            pltpu.VMEM((n_row, slots, rank_dim, w), f32),
            pltpu.VMEM((2, n_z, rank_dim, flat), f32),
            pltpu.VMEM((n_z, rank_dim, flat), f32),
            pltpu.VMEM((n_z, rank_dim, flat), f32),
            pltpu.VMEM((n_z, rank_dim, flat), f32),
            pltpu.VMEM((1, w, point_rows), f32),
            pltpu.VMEM((2, 2 * slots * w), f32),
            pltpu.VMEM((n_col, 2 * rank_dim, w), bf16),
            pltpu.VMEM((w, 2 * slots * w), bf16),
            pltpu.VMEM((w, 2 * slots * w), bf16),
            pltpu.VMEM((rank_dim, 2 * slots * w), f32),
            pltpu.VMEM((slots, 2, rank_dim, rank_dim), f32),
            pltpu.VMEM((slots, rank_dim, rank_dim), f32),
            pltpu.VMEM((rank_dim, rank_dim), f32),
            pltpu.SemaphoreType.REGULAR,
            dma((5,)), dma((slots, 2)), dma((n_col,)), dma((n_col,)),
            dma((slots, n_z)), dma((slots, n_col)), dma((slots, n_col)), dma((slots, n_col)),
            dma((slots, n_row)), dma((slots, n_row)),
            dma((3, n_col)), dma((n_col,)),
            dma((slots,)), dma((slots,)), dma((n_z,)), dma((n_z,)),
        ],
        compiler_params=pltpu.CompilerParams(
            collective_id=0, has_side_effects=True, vmem_limit_bytes=VMEM_LIMIT),
    )(*[
        pltpu.with_memory_space_constraint(value, pltpu.HBM) for value in (
            ranks.reshape(slots),
            trail_u.reshape(slots, rank_dim, width),
            trail_v.reshape(slots, rank_dim, width),
            panel_u.reshape(slots, rank_dim, w),
            panel_v.reshape(slots, rank_dim, w),
            locations.reshape(slots, 2, w),
            pend_locs,
            sketch,
        )
    ])
    kept = [pltpu.with_memory_space_constraint(value, pltpu.VMEM) for value in kept]
    pieces = 2
    return pl.pallas_call(
        functools.partial(finish, n_row),
        out_shape=(
            shape((slots, 1, 1, rank_dim, width), f32),
            shape((slots, 1, 1, rank_dim, width), f32),
            shape((slots, 1, rank_dim, w), f32),
            shape((slots, 1, rank_dim, w), f32),
        ),
        in_specs=[vmem] * 7,
        out_specs=(hbm,) * 4,
        scratch_shapes=[
            pltpu.VMEM((slots, rank_dim, width), f32),
            pltpu.VMEM((slots, rank_dim, width), f32),
            dma((slots, 2, pieces)), dma((slots, 2)),
        ],
        compiler_params=pltpu.CompilerParams(vmem_limit_bytes=VMEM_LIMIT),
    )(*kept)


def solution(mesh):
    in_specs = (
        P(None, "row", "col", None, None),
        P(None, "row", "col", None, None),
        P(None, "row", "col"),
        P(None, "row", None, "col"),
        P(None, "row", None, "col"),
        P(None, "row", None, "col"),
        P(None, "col"),
        P(),
    )
    out_specs = (
        P(None, "row", "col", None, None),
        P(None, "row", "col", None, None),
        P(None, "row", None, "col"),
        P(None, "row", None, "col"),
    )
    body = functools.partial(on_device, mesh.shape["row"], mesh.shape["col"])
    return jax.shard_map(
        body, mesh=mesh, in_specs=in_specs, out_specs=out_specs, check_vma=False
    )
```

time: 40.3 us -> 34.5 us (0.86); the launches traced: 39.7 us -> 34.3 us
  Pallas kernels: 39 us -> 33.6 us
    pallas_call x2, Pallas kernels: 39 us -> 33.6 us  [the longest x1 31.8 us: on_device(): pl.pallas_call(functools.partial(kernel, n_row, n_col), out_shape=(pltpu....]
where the time goes in v1:
time: 34.5 us; the launch traced here: 34.3 us
  Pallas kernels  33.6 us (97%)
  between operations  0.64 us (2%)
    pallas_call x1, Pallas kernels, on_device(): pl.pallas_call(functools.partial(kernel, n_row, n_col), out_shape=(pltpu....  31.8 us
    pallas_call x1, Pallas kernels, on_device(): pl.pallas_call(functools.partial(finish, n_row), out_shape=(shape((slots,...  1.79 us

profile of v1, /device:TPU:6, one launch (start us, length us, event | category | flops | bytes accessed | tf_op | source)
XLA Modules:
  0.0 34.3 jit_solution(603861581107994107)
XLA Ops:
  0.6 31.8 %shard_map.111 = (bf16[2,2,64,2048]{3,2,1,0:T(8,128)(2,1)S(1)}, bf16[2,2,64,2048]{3,2,1,0:T(8,128)(2,1)S(1)}, bf16[2,2,64,2048]{3,2,1,0:T(8,128)(2,1)S(1)}, bf16...) custom-call(s32[2]{0:T(128)} %bitcast.11, ...), custom_call_target="tpu_custom_call" | custom-call | tf_op jit(solution)/shard_map/pallas_call | solution.py:707
  32.5 1.8 %shard_map.112 = (f32[2,1,1,64,2048]{4,3,2,1,0:T(8,128)}, f32[2,1,1,64,2048]{4,3,2,1,0:T(8,128)}, f32[2,1,64,256]{3,2,1,0:T(8,128)}, f32[2,1,64,256]{3,2,1,0:T(8,128)}) custom-call(bf16[2,2,64,2048]{3,2,1,0:T(8,128)(2,1)S(1)} %get-tuple-element.11.ru, bf16[2,2,64,2048]{3,2,1,0:T(8,128)(2,1)S(1)} %get-tuple-element.12.rv, ...), custom_call_target="tpu_custom_call" | custom-call | tf_op jit(solution)/shard_map/pallas_call | solution.py:764

commit v2 on v1

--- a/solution.py
+++ b/solution.py
@@ -47,9 +47,9 @@
 
 def kernel(
     n_row, n_col,
-    ranks, trail_u, trail_v, panel_u, panel_v, locs, pend, sketch,
+    ranks_hbm, trail_u, trail_v, panel_u, panel_v, locs, pend, sketch,
     ru, rv, rp, rj, y_left, z_left, pend_acc,
-    u_buf, v_buf, sk_buf, loc_all, pu_all, pj_all, pv_all, g_part, g_peer, g_sum, g_all,
+    ranks, u_buf, v_buf, sk_buf, loc_all, pu_all, pj_all, pv_all, g_part, g_peer, g_sum, g_all,
     points, own_points, sk_both, mat_high, mat_low, acc, own_sketches, row_sketch, col_sketch,
     far_sem, load_sem, trail_sem, loc_send, loc_recv, pu_send, pf_send, pr_send, pu_recv,
     pv_send, pv_recv, pj_send, pj_recv, gx_send, gx_recv, g_send, g_recv,
@@ -67,6 +67,7 @@
     is_owner = row == owner_row
     x_row = row + 1 - 2 * (row % 2)
     y_row = (row + half_z) % n_row
+    diagonal = n_row - 1 - row
     any_active = last + row > col
 
     def active(slot):
@@ -120,7 +121,7 @@
     def pj_copy(block, way):
         src = pj_all.at[block] if way == 2 else pu_all.at[block, owner_slot]
         return remote(src, pj_all.at[block], pj_send.at[way, block], pj_recv.at[block],
-                      y_row if way == 1 else x_row, col)
+                      (x_row, y_row, x_row, diagonal)[way], col)
 
     def gx_copy(batch):
         chips = pl.ds(batch * half_z, half_z)
@@ -134,12 +135,9 @@
     def when(*terms):
         return pl.when(functools.reduce(jnp.logical_and, terms))
 
-    to_y = jnp.logical_or(wants_column(y_row), wants_column(n_row - 1 - row))
+    to_y = jnp.logical_or(wants_column(y_row), wants_column(diagonal))
     y_of_owner = row == (owner_row + half_z) % n_row
     is_relay = jnp.logical_and(y_of_owner, wants_column(x_row))
-    takes_column = jnp.logical_and(
-        jnp.logical_not(is_owner),
-        jnp.logical_or(wants_column(row), is_relay))
 
     barrier = pltpu.get_barrier_semaphore()
 
@@ -161,6 +159,7 @@
         pltpu.make_async_copy(panel_v, pv_all.at[row], load_sem.at[2]),
         pltpu.make_async_copy(panel_u, pu_all.at[col], load_sem.at[3]),
         pltpu.make_async_copy(sketch, sk_buf, load_sem.at[4]),
+        pltpu.make_async_copy(ranks_hbm, ranks, load_sem.at[5]),
     ]
     for load in loads:
         load.start()
@@ -175,68 +174,8 @@
             trail_load(slot, 0).start()
             trail_load(slot, 1).start()
 
-    for load in loads[:4]:
+    for load in loads:
         load.wait()
-    pl.semaphore_wait(barrier, n_row + 2 * z)
-
-    for chip in range(n_z - 1):
-        @pl.when(z > chip)
-        def _(chip=chip):
-            hello(far_sem, row, 2 * chip)
-            hello(far_sem, row, 2 * chip + 1)
-
-    def each_loc(act, higher):
-        for chip in range(n_z):
-            @pl.when(z < chip if higher else z > chip)
-            def _(chip=chip):
-                act(loc_copy(col, 2 * chip))
-                act(loc_copy(col, 2 * chip + 1))
-
-    def each_direct(act, higher, slot):
-        for chip in (range(1, n_z) if higher else reversed(range(n_z - 1))):
-            @when(z < chip if higher else z > chip, direct(slot, chip, z))
-            def _(chip=chip):
-                act(pu_direct(slot, chip))
-
-    def each_pv(act, slot):
-        for step in range(1, n_row):
-            target = (row + step) % n_row
-
-            @pl.when(last + target > slot * n_row + row)
-            def _(target=target):
-                act(pv_copy(slot, row, target))
-
-    def each_column(act, block, slot=None):
-        ours = is_owner if slot is None else jnp.logical_and(is_owner, owner_slot == slot)
-
-        @when(ours, wants_column(x_row))
-        def _():
-            act(pj_copy(block, 0))
-
-        @when(ours, to_y)
-        def _():
-            act(pj_copy(block, 1))
-
-    def start(copy):
-        copy.start()
-
-    def wait_send(copy):
-        copy.wait_send()
-
-    start(loc_copy(col, partner))
-    each_loc(start, False)
-    each_pv(start, 0)
-    for slot in range(slots):
-        each_direct(start, False, slot)
-
-        @pl.when(needs(slot, z))
-        def _(slot=slot):
-            start(pu_partner(slot, col))
-    each_column(start, col)
-    for slot in range(1, slots):
-        each_pv(start, slot)
-
-    loads[4].wait()
     sk_high, sk_low = halves(sk_buf[...])
     for block in range(n_col):
         sk_both[block, 0:rank_dim] = sk_high[:, block * w:(block + 1) * w]
@@ -319,6 +258,75 @@
             def _(slot=slot):
                 own_sketch(slot)
 
+    corner = (n_row - row) // n_row
+    pl.loop(0, corner)(chunk)
+
+    @pl.when(corner == 1)
+    def _():
+        own_all()
+    pl.semaphore_wait(barrier, n_row + 2 * z)
+
+    for chip in range(n_z - 1):
+        @pl.when(z > chip)
+        def _(chip=chip):
+            hello(far_sem, row, 2 * chip)
+            hello(far_sem, row, 2 * chip + 1)
+
+    def each_loc(act, higher):
+        for chip in range(n_z):
+            @pl.when(z < chip if higher else z > chip)
+            def _(chip=chip):
+                act(loc_copy(col, 2 * chip))
+                act(loc_copy(col, 2 * chip + 1))
+
+    def each_direct(act, higher, slot):
+        for chip in (range(1, n_z) if higher else reversed(range(n_z - 1))):
+            @when(z < chip if higher else z > chip, direct(slot, chip, z))
+            def _(chip=chip):
+                act(pu_direct(slot, chip))
+
+    def each_pv(act, slot):
+        for step in range(1, n_row):
+            target = (row + step) % n_row
+
+            @pl.when(last + target > slot * n_row + row)
+            def _(target=target):
+                act(pv_copy(slot, row, target))
+
+    def each_column(act, block, step, slot=None):
+        ours = is_owner if slot is None else jnp.logical_and(is_owner, owner_slot == slot)
+        final = step == n_z - 1
+
+        @when(ours, wants_column(x_row))
+        def _():
+            act(pj_copy(block, 0))
+
+        @when(ours, wants_column(y_row) if final else to_y)
+        def _():
+            act(pj_copy(block, 1))
+
+        if final:
+            @when(ours, wants_column(diagonal))
+            def _():
+                act(pj_copy(block, 3))
+
+    def start(copy):
+        copy.start()
+
+    def wait_send(copy):
+        copy.wait_send()
+
+    def send_lower(slot):
+        each_direct(start, False, slot)
+
+        @pl.when(needs(slot, z))
+        def _():
+            start(pu_partner(slot, col))
+
+    start(loc_copy(col, partner))
+    each_loc(start, False)
+    each_pv(start, 0)
+    send_lower(0)
     def arrive(slot, step):
         chip = chip_at(step)
         block = 2 * chip + core
@@ -334,27 +342,46 @@
             @pl.when(needs(slot, z))
             def _():
                 pu_partner(slot, block).start()
-            each_column(start, block, slot)
+            each_column(start, block, step, slot)
+
+    def spreads(slot):
+        return jnp.logical_and(is_owner, owner_slot == slot)
 
     def from_partner(slot, step):
         block = 2 * chip_at(step) + other
 
-        @pl.when(needs(slot, z))
+        @when(needs(slot, z), spreads(slot))
         def _():
             pu_partner(slot, block).wait_recv()
-            each_column(start, block, slot)
+            each_column(start, block, step, slot)
+
+    def settle_rows(slot, first, final):
+        @when(needs(slot, z), jnp.logical_not(spreads(slot)))
+        def _():
+            for step in range(first, final):
+                pu_partner(slot, 2 * chip_at(step) + other).wait_recv()
+        absorb_rows(slot, first, final)
+
+    def pair(step):
+        return [2 * chip_at(step) + (core + flip) % 2 for flip in range(2)]
 
     def column(step):
-        for flip in range(2):
-            block = 2 * chip_at(step) + (core + flip) % 2
-
-            @pl.when(takes_column)
-            def _():
+        @pl.when(is_relay)
+        def _():
+            for block in pair(step):
                 pj_copy(block, 0).wait_recv()
-
-                @pl.when(is_relay)
-                def _():
-                    pj_copy(block, 2).start()
+                pj_copy(block, 2).start()
+
+    def settle_column(first, final):
+        for step in range(first, final):
+            late = step == n_z - 1
+
+            @when(jnp.logical_not(is_owner), wants_column(row),
+                  True if late else jnp.logical_not(is_relay))
+            def _(step=step):
+                for block in pair(step):
+                    pj_copy(block, 0).wait_recv()
+        absorb_column(first, final)
 
     def gram_part(slot):
         own_v = pv_all[row].reshape(slots * rank_dim, w)
@@ -432,55 +459,72 @@
         for slot in range(slots):
             each_direct(start, True, slot)
 
-    chunks(0, 2)
-    own_all()
+    pl.loop(corner, 2)(chunk)
+    for slot in range(1, slots):
+        send_lower(slot)
+
+    @pl.when(corner == 0)
+    def _():
+        own_all()
     upward()
+    arrive(0, 1)
+    each_column(start, col, 0)
+    from_partner(0, 0)
+    chunks(2, 3)
+    gram_part(0)
+    for slot in range(1, slots):
+        each_pv(start, slot)
+    arrive(0, 2)
+    gram_swap(0)
+    from_partner(0, 1)
+    chunks(3, 4)
+    gram_sum(0)
+    for slot in range(1, slots):
+        arrive(slot, 1)
+        from_partner(slot, 0)
+    each_gram(start, 0)
+    column(0)
+    chunks(4, 5)
+    for slot in range(1, slots):
+        arrive(slot, 2)
+    arrive(0, 3)
+    from_partner(0, 2)
+    for slot in range(1, slots):
+        from_partner(slot, 1)
+    column(1)
+    chunks(5, 6)
+    from_partner(0, 3)
+    for slot in range(1, slots):
+        from_partner(slot, 2)
+    column(2)
+    for slot in range(1, slots):
+        gram_part(slot)
+    settle_rows(0, 0, n_z - 1)
+    for slot in range(1, slots):
+        gram_swap(slot)
+    chunks(6, 7)
+    for slot in range(1, slots):
+        arrive(slot, 3)
+        gram_sum(slot)
+    chunks(7, 8)
+    for slot in range(1, slots):
+        each_gram(start, slot)
+        from_partner(slot, 3)
+        settle_rows(slot, 0, n_z - 1)
+    settle_rows(0, n_z - 1, n_z)
+    settle_column(0, n_z - 1)
+    pend_acc[...] = acc[...] * matern_scale
+
+    wait_send(loc_copy(col, partner))
+    for higher in (False, True):
+        each_loc(wait_send, higher)
+        for slot in range(slots):
+            each_direct(wait_send, higher, slot)
     for slot in range(slots):
-        from_partner(slot, 0)
-    gram_part(0)
-    for slot in range(slots):
-        arrive(slot, 1)
-    column(0)
-    gram_swap(0)
-    chunks(2, 3)
-    gram_sum(0)
-    for slot in range(slots):
-        from_partner(slot, 1)
-    arrive(0, 2)
-    each_gram(start, 0)
-    chunks(3, 4)
-    for slot in range(1, slots):
-        arrive(slot, 2)
-    column(1)
-    for slot in range(1, slots):
-        gram_part(slot)
-    from_partner(0, 2)
-    chunks(4, 5)
-    for slot in range(1, slots):
-        gram_swap(slot)
-    for slot in range(1, slots):
-        from_partner(slot, 2)
-    arrive(0, 3)
-    column(2)
-    chunks(5, 6)
-    for slot in range(1, slots):
-        gram_sum(slot)
-    for slot in range(1, slots):
-        arrive(slot, 3)
-    from_partner(0, 3)
-    for slot in range(slots):
-        absorb_rows(slot, 0, n_z - 1)
-    for slot in range(1, slots):
-        each_gram(start, slot)
-    absorb_column(0, n_z - 1)
-    chunks(6, 8)
-    pend_acc[...] = acc[...] * matern_scale
-    column(3)
-    for slot in range(1, slots):
-        from_partner(slot, 3)
-    for slot in range(slots):
-        absorb_rows(slot, n_z - 1, n_z)
-    absorb_column(n_z - 1, n_z)
+        each_pv(wait_send, slot)
+    settle_column(n_z - 1, n_z)
+    for slot in range(1, slots):
+        settle_rows(slot, n_z - 1, n_z)
 
     @pl.when(any_active)
     def _():
@@ -509,37 +553,30 @@
                 z_left[slot] = stacked(
                     jnp.concatenate([own_sketches[slot, 1], -right_core], axis=1))
 
-    wait_send(loc_copy(col, partner))
-    for higher in (False, True):
-        each_loc(wait_send, higher)
-        for slot in range(slots):
-            each_direct(wait_send, higher, slot)
     for slot in range(slots):
-        each_pv(wait_send, slot)
         each_gram(wait_send, slot)
 
         @pl.when(has_batch(slot))
         def _(slot=slot):
             gx_copy(slot).wait_send()
         for step in range(n_z):
-            chip = chip_at(step)
-            block = 2 * chip + core
+            block = 2 * chip_at(step) + core
 
             @pl.when(needs(slot, z))
             def _(slot=slot, block=block):
                 pu_partner(slot, block).wait_send()
 
-            @when(z == 1, chip >= 2)
+            @when(z == 1, chip_at(step) >= 2)
             def _(slot=slot, block=block):
                 pu_relay(slot, block).wait_send()
-
-    @pl.loop(0, n_col)
-    def _(block):
-        each_column(wait_send, block)
-
-        @pl.when(is_relay)
-        def _():
-            pj_copy(block, 2).wait_send()
+    for step in range(n_z):
+        for block in pair(step):
+            each_column(wait_send, block, step)
+        if step < n_z - 1:
+            @pl.when(is_relay)
+            def _(step=step):
+                for block in pair(step):
+                    pj_copy(block, 2).wait_send()
 
 
 def finish(
@@ -701,7 +738,6 @@
     dma = pltpu.SemaphoreType.DMA
     vmem = pl.BlockSpec(memory_space=pltpu.VMEM)
     hbm = pl.BlockSpec(memory_space=pltpu.HBM)
-    smem = pl.BlockSpec(memory_space=pltpu.SMEM)
     point_rows = -(-(2 * slots + 2) // 8) * 8
     shape = jax.ShapeDtypeStruct
     kept = pl.pallas_call(
@@ -715,9 +751,10 @@
             pltpu.VMEM((slots, 2 * rank_dim, 4 * rank_dim), bf16),
             pltpu.VMEM((rank_dim, 2 * slots * w), f32),
         ),
-        in_specs=[smem] + [hbm] * 7,
+        in_specs=[hbm] * 8,
         out_specs=(vmem,) * 7,
         scratch_shapes=[
+            pltpu.SMEM((slots,), jnp.int32),
             pltpu.VMEM((slots, rank_dim, width), f32),
             pltpu.VMEM((slots, rank_dim, width), f32),
             pltpu.VMEM((rank_dim, width), f32),
@@ -739,10 +776,10 @@
             pltpu.VMEM((slots, rank_dim, rank_dim), f32),
             pltpu.VMEM((rank_dim, rank_dim), f32),
             pltpu.SemaphoreType.REGULAR,
-            dma((5,)), dma((slots, 2)), dma((n_col,)), dma((n_col,)),
+            dma((6,)), dma((slots, 2)), dma((n_col,)), dma((n_col,)),
             dma((slots, n_z)), dma((slots, n_col)), dma((slots, n_col)), dma((slots, n_col)),
             dma((slots, n_row)), dma((slots, n_row)),
-            dma((3, n_col)), dma((n_col,)),
+            dma((4, n_col)), dma((n_col,)),
             dma((slots,)), dma((slots,)), dma((n_z,)), dma((n_z,)),
         ],
         compiler_params=pltpu.CompilerParams(

time: 34.5 us -> 31 us (0.90)
  the two profiles are of different devices: /device:TPU:6 before, /device:TPU:5 now
where the time goes in v2:
time: 31 us; the launch traced here: 30.8 us
  Pallas kernels  30.2 us (97%)
  between operations  0.64 us (2%)
    pallas_call x1, Pallas kernels, on_device(): pl.pallas_call(functools.partial(kernel, n_row, n_col), out_shape=(pltpu....  28.4 us
    pallas_call x1, Pallas kernels, on_device(): pl.pallas_call(functools.partial(finish, n_row), out_shape=(shape((slots,...  1.78 us

profile of v2, /device:TPU:5, one launch (start us, length us, event | category | flops | bytes accessed | tf_op | source)
XLA Modules:
  0.0 30.8 jit_solution(9741697358618489735)
XLA Ops:
  0.6 28.4 %shard_map.111 = (bf16[2,2,64,2048]{3,2,1,0:T(8,128)(2,1)S(1)}, bf16[2,2,64,2048]{3,2,1,0:T(8,128)(2,1)S(1)}, bf16[2,2,64,2048]{3,2,1,0:T(8,128)(2,1)S(1)}, bf16...) custom-call(s32[2]{0:T(128)} %bitcast.11, ...), custom_call_target="tpu_custom_call" | custom-call | tf_op jit(solution)/shard_map/pallas_call | solution.py:743
  29.0 1.8 %shard_map.112 = (f32[2,1,1,64,2048]{4,3,2,1,0:T(8,128)}, f32[2,1,1,64,2048]{4,3,2,1,0:T(8,128)}, f32[2,1,64,256]{3,2,1,0:T(8,128)}, f32[2,1,64,256]{3,2,1,0:T(8,128)}) custom-call(bf16[2,2,64,2048]{3,2,1,0:T(8,128)(2,1)S(1)} %get-tuple-element.11.ru, bf16[2,2,64,2048]{3,2,1,0:T(8,128)(2,1)S(1)} %get-tuple-element.12.rv, ...), custom_call_target="tpu_custom_call" | custom-call | tf_op jit(solution)/shard_map/pallas_call | solution.py:801

commit v3 on v2

--- a/solution.py
+++ b/solution.py
@@ -326,7 +326,15 @@
     start(loc_copy(col, partner))
     each_loc(start, False)
     each_pv(start, 0)
-    send_lower(0)
+
+    @pl.when(z < n_z - 1)
+    def _():
+        send_lower(0)
+
+    @pl.when(z == 1)
+    def _():
+        for slot in range(1, slots):
+            send_lower(slot)
     def arrive(slot, step):
         chip = chip_at(step)
         block = 2 * chip + core
@@ -459,56 +467,84 @@
         for slot in range(slots):
             each_direct(start, True, slot)
 
-    pl.loop(corner, 2)(chunk)
-    for slot in range(1, slots):
-        send_lower(slot)
+    def early(slot, step):
+        @pl.when(z > 0)
+        def _():
+            arrive(slot, step)
+
+    def late(slot, step):
+        @pl.when(z == 0)
+        def _():
+            arrive(slot, step)
+
+    top = n_z - 1
+    pl.loop(corner, 1)(chunk)
+
+    @pl.when(z == top)
+    def _():
+        send_lower(0)
+    chunks(1, 2)
+
+    @when(z != 1, z < top)
+    def _():
+        for slot in range(1, slots):
+            send_lower(slot)
+    for slot in range(1, slots):
+        each_pv(start, slot)
+    each_column(start, col, 0)
 
     @pl.when(corner == 0)
     def _():
         own_all()
     upward()
-    arrive(0, 1)
-    each_column(start, col, 0)
+
+    @pl.when(z == top)
+    def _():
+        for slot in range(1, slots):
+            send_lower(slot)
     from_partner(0, 0)
     chunks(2, 3)
+    for slot in range(1, slots):
+        from_partner(slot, 0)
+    arrive(0, 1)
     gram_part(0)
-    for slot in range(1, slots):
-        each_pv(start, slot)
-    arrive(0, 2)
+    from_partner(0, 1)
+    early(0, 2)
     gram_swap(0)
-    from_partner(0, 1)
     chunks(3, 4)
     gram_sum(0)
     for slot in range(1, slots):
-        arrive(slot, 1)
-        from_partner(slot, 0)
+        early(slot, 1)
+    column(0)
     each_gram(start, 0)
-    column(0)
     chunks(4, 5)
     for slot in range(1, slots):
-        arrive(slot, 2)
-    arrive(0, 3)
-    from_partner(0, 2)
-    for slot in range(1, slots):
+        gram_part(slot)
+        early(slot, 2)
         from_partner(slot, 1)
+    late(0, 2)
+    for slot in range(1, slots):
+        gram_swap(slot)
     column(1)
     chunks(5, 6)
+    for slot in range(1, slots):
+        gram_sum(slot)
+        late(slot, 1)
+        from_partner(slot, 2)
+    from_partner(0, 2)
+    for slot in range(1, slots):
+        each_gram(start, slot)
+    arrive(0, 3)
+    chunks(6, 7)
+    column(2)
+    for slot in range(1, slots):
+        late(slot, 2)
+        early(slot, 3)
     from_partner(0, 3)
-    for slot in range(1, slots):
-        from_partner(slot, 2)
-    column(2)
-    for slot in range(1, slots):
-        gram_part(slot)
     settle_rows(0, 0, n_z - 1)
-    for slot in range(1, slots):
-        gram_swap(slot)
-    chunks(6, 7)
-    for slot in range(1, slots):
-        arrive(slot, 3)
-        gram_sum(slot)
     chunks(7, 8)
     for slot in range(1, slots):
-        each_gram(start, slot)
+        late(slot, 3)
         from_partner(slot, 3)
         settle_rows(slot, 0, n_z - 1)
     settle_rows(0, n_z - 1, n_z)
@@ -520,8 +556,39 @@
         each_loc(wait_send, higher)
         for slot in range(slots):
             each_direct(wait_send, higher, slot)
+
+    def forwards_done(slot, first, final):
+        for step in range(first, final):
+            block = 2 * chip_at(step) + core
+
+            @pl.when(needs(slot, z))
+            def _(block=block):
+                pu_partner(slot, block).wait_send()
+
+            @when(z == 1, chip_at(step) >= 2)
+            def _(block=block):
+                pu_relay(slot, block).wait_send()
+
+    def columns_done(step):
+        for block in pair(step):
+            each_column(wait_send, block, step)
+        if step < n_z - 1:
+            @pl.when(is_relay)
+            def _():
+                for block in pair(step):
+                    pj_copy(block, 2).wait_send()
+
     for slot in range(slots):
         each_pv(wait_send, slot)
+
+        @pl.when(has_batch(slot))
+        def _(slot=slot):
+            gx_copy(slot).wait_send()
+        each_gram(wait_send, slot)
+        forwards_done(slot, 0, n_z - 1)
+    forwards_done(0, n_z - 1, n_z)
+    for step in range(n_z - 1):
+        columns_done(step)
     settle_column(n_z - 1, n_z)
     for slot in range(1, slots):
         settle_rows(slot, n_z - 1, n_z)
@@ -553,30 +620,9 @@
                 z_left[slot] = stacked(
                     jnp.concatenate([own_sketches[slot, 1], -right_core], axis=1))
 
-    for slot in range(slots):
-        each_gram(wait_send, slot)
-
-        @pl.when(has_batch(slot))
-        def _(slot=slot):
-            gx_copy(slot).wait_send()
-        for step in range(n_z):
-            block = 2 * chip_at(step) + core
-
-            @pl.when(needs(slot, z))
-            def _(slot=slot, block=block):
-                pu_partner(slot, block).wait_send()
-
-            @when(z == 1, chip_at(step) >= 2)
-            def _(slot=slot, block=block):
-                pu_relay(slot, block).wait_send()
-    for step in range(n_z):
-        for block in pair(step):
-            each_column(wait_send, block, step)
-        if step < n_z - 1:
-            @pl.when(is_relay)
-            def _(step=step):
-                for block in pair(step):
-                    pj_copy(block, 2).wait_send()
+    for slot in range(1, slots):
+        forwards_done(slot, n_z - 1, n_z)
+    columns_done(n_z - 1)
 
 
 def finish(

time: 31 us -> 26.4 us (0.85)
  the two profiles are of different devices: /device:TPU:5 before, /device:TPU:6 now
where the time goes in v3:
time: 26.4 us; the launch traced here: 26.3 us
  Pallas kernels  25.6 us (97%)
  between operations  0.64 us (2%)
    pallas_call x1, Pallas kernels, on_device(): pl.pallas_call(functools.partial(kernel, n_row, n_col), out_shape=(pltpu....  23.8 us
    pallas_call x1, Pallas kernels, on_device(): pl.pallas_call(functools.partial(finish, n_row), out_shape=(shape((slots,...  1.79 us

profile of v3, /device:TPU:6, one launch (start us, length us, event | category | flops | bytes accessed | tf_op | source)
XLA Modules:
  0.0 26.3 jit_solution(14002737495678713250)
XLA Ops:
  0.6 23.8 %shard_map.111 = (bf16[2,2,64,2048]{3,2,1,0:T(8,128)(2,1)S(1)}, bf16[2,2,64,2048]{3,2,1,0:T(8,128)(2,1)S(1)}, bf16[2,2,64,2048]{3,2,1,0:T(8,128)(2,1)S(1)}, bf16...) custom-call(s32[2]{0:T(128)} %bitcast.11, ...), custom_call_target="tpu_custom_call" | custom-call | tf_op jit(solution)/shard_map/pallas_call | solution.py:789
  24.5 1.8 %shard_map.112 = (f32[2,1,1,64,2048]{4,3,2,1,0:T(8,128)}, f32[2,1,1,64,2048]{4,3,2,1,0:T(8,128)}, f32[2,1,64,256]{3,2,1,0:T(8,128)}, f32[2,1,64,256]{3,2,1,0:T(8,128)}) custom-call(bf16[2,2,64,2048]{3,2,1,0:T(8,128)(2,1)S(1)} %get-tuple-element.11.ru, bf16[2,2,64,2048]{3,2,1,0:T(8,128)(2,1)S(1)} %get-tuple-element.12.rv, ...), custom_call_target="tpu_custom_call" | custom-call | tf_op jit(solution)/shard_map/pallas_call | solution.py:847

commit v4 on v3

--- a/solution.py
+++ b/solution.py
@@ -19,7 +19,6 @@
 NN = (((1,), (0,)), ((), ()))
 NT = (((1,), (1,)), ((), ()))
 SLAB = 16
-UNROLL = 8
 VMEM_LIMIT = 32 << 20
 
 
@@ -76,14 +75,13 @@
     def needs(slot, chip):
         return 2 * chip <= slot * n_row + row
 
-    def carries(slot, chip, source):
-        return jnp.logical_or(
-            needs(slot, chip), jnp.logical_and(chip == 1, source >= 2))
-
     def direct(slot, chip, source):
+        near = jnp.logical_or(chip > 0, source < 2)
         return jnp.logical_and(
-            carries(slot, chip, source),
-            jnp.logical_or(chip > 0, source < 2))
+            needs(slot, chip), jnp.logical_or(near, jnp.logical_not(needs(slot, 1))))
+
+    def hosts(slot):
+        return (slot * n_row + row) // 2 == z
 
     def chip_at(step):
         over = (z + step) // n_z
@@ -204,13 +202,13 @@
             stack.append(jnp.zeros((pad_rows, w), jnp.float32))
         points[0] = jnp.concatenate(stack, axis=0).T * point_scale
 
-        @pl.loop(0, w // SLAB, unroll=UNROLL)
-        def _(slab):
-            rows = pl.ds(pl.multiple_of(slab * SLAB, SLAB), SLAB)
-            at = points[0, rows, :]
-            for part in range(2 * slots):
-                base = 2 * slots if part < slots else 2 * (part - slots)
-                lanes = slice(part * w, (part + 1) * w)
+        sk = sk_both[block]
+        for part in range(2 * slots):
+            base = 2 * slots if part < slots else 2 * (part - slots)
+            lanes = slice(part * w, (part + 1) * w)
+            for slab in range(w // SLAB):
+                rows = slice(slab * SLAB, (slab + 1) * SLAB)
+                at = points[0, rows, :]
                 delta_x = at[:, base:base + 1] - own_points[0:1, lanes]
                 delta_y = at[:, base + 1:base + 2] - own_points[1:2, lanes]
                 square = delta_x * delta_x + delta_y * delta_y
@@ -219,11 +217,9 @@
                 high, low = halves(value)
                 mat_high[rows, lanes] = high
                 mat_low[rows, lanes] = low
-
-        sk = sk_both[block]
-        both = product(sk, mat_high[...], NN)
-        acc[...] += (both[:rank_dim] + both[rank_dim:]
-                     + product(sk[:rank_dim], mat_low[...], NN))
+            both = product(sk, mat_high[:, lanes], NN)
+            acc[:, lanes] += (both[:rank_dim] + both[rank_dim:]
+                              + product(sk[:rank_dim], mat_low[:, lanes], NN))
 
     def chunks(first, final):
         pl.loop(first * n_col // 8, final * n_col // 8)(chunk)
@@ -293,20 +289,25 @@
             def _(target=target):
                 act(pv_copy(slot, row, target))
 
+    def straight(step):
+        if step == n_z - 1:
+            return True
+        return False
+
     def each_column(act, block, step, slot=None):
         ours = is_owner if slot is None else jnp.logical_and(is_owner, owner_slot == slot)
-        final = step == n_z - 1
+        far = straight(step)
 
         @when(ours, wants_column(x_row))
         def _():
             act(pj_copy(block, 0))
 
-        @when(ours, wants_column(y_row) if final else to_y)
+        @when(ours, wants_column(y_row) if far is True else to_y)
         def _():
             act(pj_copy(block, 1))
 
-        if final:
-            @when(ours, wants_column(diagonal))
+        if far is not False:
+            @when(ours, wants_column(diagonal), far)
             def _():
                 act(pj_copy(block, 3))
 
@@ -331,7 +332,7 @@
     def _():
         send_lower(0)
 
-    @pl.when(z == 1)
+    @when(z == 1, needs(0, z))
     def _():
         for slot in range(1, slots):
             send_lower(slot)
@@ -339,17 +340,14 @@
         chip = chip_at(step)
         block = 2 * chip + core
 
-        @pl.when(carries(slot, z, chip))
+        @pl.when(needs(slot, z))
         def _():
             pu_partner(slot, block).wait_recv()
 
             @when(z == 1, chip >= 2)
             def _():
                 pu_relay(slot, block).start()
-
-            @pl.when(needs(slot, z))
-            def _():
-                pu_partner(slot, block).start()
+            pu_partner(slot, block).start()
             each_column(start, block, step, slot)
 
     def spreads(slot):
@@ -378,7 +376,10 @@
         def _():
             for block in pair(step):
                 pj_copy(block, 0).wait_recv()
-                pj_copy(block, 2).start()
+
+                @pl.when(jnp.logical_not(straight(step)))
+                def _(block=block):
+                    pj_copy(block, 2).start()
 
     def settle_column(first, final):
         for step in range(first, final):
@@ -468,12 +469,12 @@
             each_direct(start, True, slot)
 
     def early(slot, step):
-        @pl.when(z > 0)
+        @pl.when(jnp.logical_or(z > 0, hosts(slot)))
         def _():
             arrive(slot, step)
 
     def late(slot, step):
-        @pl.when(z == 0)
+        @when(z == 0, jnp.logical_not(hosts(slot)))
         def _():
             arrive(slot, step)
 
@@ -498,7 +499,7 @@
         own_all()
     upward()
 
-    @pl.when(z == top)
+    @pl.when(jnp.logical_or(z == top, jnp.logical_and(z == 1, jnp.logical_not(needs(0, z)))))
     def _():
         for slot in range(1, slots):
             send_lower(slot)
@@ -506,49 +507,60 @@
     chunks(2, 3)
     for slot in range(1, slots):
         from_partner(slot, 0)
-    arrive(0, 1)
+    @pl.when(z > 0)
+    def _():
+        arrive(0, 1)
     gram_part(0)
-    from_partner(0, 1)
-    early(0, 2)
+
+    @pl.when(z > 0)
+    def _():
+        arrive(0, 2)
     gram_swap(0)
     chunks(3, 4)
+
+    @pl.when(z == 0)
+    def _():
+        arrive(0, 1)
     gram_sum(0)
+    from_partner(0, 1)
     for slot in range(1, slots):
         early(slot, 1)
-    column(0)
+
+    @when(z == 0, hosts(0))
+    def _():
+        arrive(0, 2)
     each_gram(start, 0)
     chunks(4, 5)
     for slot in range(1, slots):
-        gram_part(slot)
         early(slot, 2)
         from_partner(slot, 1)
-    late(0, 2)
+        gram_part(slot)
+    from_partner(0, 2)
+    column(0)
     for slot in range(1, slots):
         gram_swap(slot)
-    column(1)
+    early(0, 3)
     chunks(5, 6)
     for slot in range(1, slots):
         gram_sum(slot)
         late(slot, 1)
         from_partner(slot, 2)
-    from_partner(0, 2)
+    late(0, 2)
+    from_partner(0, 3)
     for slot in range(1, slots):
         each_gram(start, slot)
-    arrive(0, 3)
     chunks(6, 7)
+    for slot in range(1, slots):
+        early(slot, 3)
+    column(1)
+    chunks(7, 8)
+    for slot in range(1, slots):
+        settle_rows(slot, 0, n_z - 2)
+    late(0, 3)
     column(2)
     for slot in range(1, slots):
         late(slot, 2)
-        early(slot, 3)
-    from_partner(0, 3)
-    settle_rows(0, 0, n_z - 1)
-    chunks(7, 8)
-    for slot in range(1, slots):
-        late(slot, 3)
-        from_partner(slot, 3)
-        settle_rows(slot, 0, n_z - 1)
-    settle_rows(0, n_z - 1, n_z)
-    settle_column(0, n_z - 1)
+    settle_rows(0, 0, n_z)
     pend_acc[...] = acc[...] * matern_scale
 
     wait_send(loc_copy(col, partner))
@@ -565,7 +577,7 @@
             def _(block=block):
                 pu_partner(slot, block).wait_send()
 
-            @when(z == 1, chip_at(step) >= 2)
+            @when(z == 1, chip_at(step) >= 2, needs(slot, z))
             def _(block=block):
                 pu_relay(slot, block).wait_send()
 
@@ -573,7 +585,7 @@
         for block in pair(step):
             each_column(wait_send, block, step)
         if step < n_z - 1:
-            @pl.when(is_relay)
+            @when(is_relay, jnp.logical_not(straight(step)))
             def _():
                 for block in pair(step):
                     pj_copy(block, 2).wait_send()
@@ -589,9 +601,13 @@
     forwards_done(0, n_z - 1, n_z)
     for step in range(n_z - 1):
         columns_done(step)
+    for slot in range(1, slots):
+        late(slot, 3)
+        from_partner(slot, 3)
+    settle_column(0, n_z - 1)
+    for slot in range(1, slots):
+        settle_rows(slot, n_z - 2, n_z)
     settle_column(n_z - 1, n_z)
-    for slot in range(1, slots):
-        settle_rows(slot, n_z - 1, n_z)
 
     @pl.when(any_active)
     def _():

time: 26.4 us -> 24.6 us (0.932)
  Pallas kernels: 25.6 us -> 23.6 us
    pallas_call x1, Pallas kernels: 23.8 us -> 21.9 us  [on_device(): pl.pallas_call(functools.partial(kernel, n_row, n_col), out_shape=(pltpu....]
where the time goes in v4:
time: 24.6 us; the launch traced here: 24.3 us
  Pallas kernels  23.6 us (96%)
  between operations  0.64 us (3%)
    pallas_call x1, Pallas kernels, on_device(): pl.pallas_call(functools.partial(kernel, n_row, n_col), out_shape=(pltpu....  21.9 us
    pallas_call x1, Pallas kernels, on_device(): pl.pallas_call(functools.partial(finish, n_row), out_shape=(shape((slots,...  1.8 us

profile of v4, /device:TPU:6, one launch (start us, length us, event | category | flops | bytes accessed | tf_op | source)
XLA Modules:
  0.0 24.3 jit_solution(12960662615690905935)
XLA Ops:
  0.6 21.9 %shard_map.111 = (bf16[2,2,64,2048]{3,2,1,0:T(8,128)(2,1)S(1)}, bf16[2,2,64,2048]{3,2,1,0:T(8,128)(2,1)S(1)}, bf16[2,2,64,2048]{3,2,1,0:T(8,128)(2,1)S(1)}, bf16...) custom-call(s32[2]{0:T(128)} %bitcast.11, ...), custom_call_target="tpu_custom_call" | custom-call | tf_op jit(solution)/shard_map/pallas_call | solution.py:805
  22.5 1.8 %shard_map.112 = (f32[2,1,1,64,2048]{4,3,2,1,0:T(8,128)}, f32[2,1,1,64,2048]{4,3,2,1,0:T(8,128)}, f32[2,1,64,256]{3,2,1,0:T(8,128)}, f32[2,1,64,256]{3,2,1,0:T(8,128)}) custom-call(bf16[2,2,64,2048]{3,2,1,0:T(8,128)(2,1)S(1)} %get-tuple-element.11.ru, bf16[2,2,64,2048]{3,2,1,0:T(8,128)(2,1)S(1)} %get-tuple-element.12.rv, ...), custom_call_target="tpu_custom_call" | custom-call | tf_op jit(solution)/shard_map/pallas_call | solution.py:863

commit v5 on v4

--- a/solution.py
+++ b/solution.py
@@ -49,8 +49,8 @@
     ranks_hbm, trail_u, trail_v, panel_u, panel_v, locs, pend, sketch,
     ru, rv, rp, rj, y_left, z_left, pend_acc,
     ranks, u_buf, v_buf, sk_buf, loc_all, pu_all, pj_all, pv_all, g_part, g_peer, g_sum, g_all,
-    points, own_points, sk_both, mat_high, mat_low, acc, own_sketches, row_sketch, col_sketch,
-    far_sem, load_sem, trail_sem, loc_send, loc_recv, pu_send, pf_send, pr_send, pu_recv,
+    points, own_points, sk_both, mat_high, mat_low, acc, own_sketches, row_sketch, col_sketch, gram_all,
+    far_sem, load_sem, trail_sem, loc_send, lf_send, loc_recv, pu_send, pf_send, pr_send, pu_recv,
     pv_send, pv_recv, pj_send, pj_recv, gx_send, gx_recv, g_send, g_recv,
 ):
     row, col = lax.axis_index("row"), lax.axis_index("col")
@@ -83,6 +83,10 @@
     def hosts(slot):
         return (slot * n_row + row) // 2 == z
 
+    host_slot = 2 * z // n_row
+    host_col = host_slot * n_row + row
+    is_host = host_col // 2 == z
+
     def chip_at(step):
         over = (z + step) // n_z
         return z + step + over * (n_z - 1 - 2 * step - z)
@@ -99,6 +103,10 @@
         return remote(loc_all.at[source], loc_all.at[source], loc_send.at[target],
                       loc_recv.at[source], row, target)
 
+    def loc_forward(block):
+        return remote(loc_all.at[block], loc_all.at[block], lf_send.at[block],
+                      loc_recv.at[block], row, partner)
+
     def pv_copy(slot, source, target):
         return remote(pv_all.at[source, slot], pv_all.at[source, slot],
                       pv_send.at[slot, target], pv_recv.at[slot, source], target, col)
@@ -117,9 +125,9 @@
         return pu_copy(slot, block, pr_send.at[slot, block], core)
 
     def pj_copy(block, way):
-        src = pj_all.at[block] if way == 2 else pu_all.at[block, owner_slot]
+        src = pj_all.at[block] if way == 2 else pu_all.at[block, host_slot]
         return remote(src, pj_all.at[block], pj_send.at[way, block], pj_recv.at[block],
-                      (x_row, y_row, x_row, diagonal)[way], col)
+                      (x_row, y_row, x_row, diagonal)[way], col if way == 2 else host_col)
 
     def gx_copy(batch):
         chips = pl.ds(batch * half_z, half_z)
@@ -133,7 +141,10 @@
     def when(*terms):
         return pl.when(functools.reduce(jnp.logical_and, terms))
 
-    to_y = jnp.logical_or(wants_column(y_row), wants_column(diagonal))
+    def host_wants(at_row):
+        return last + at_row > host_col
+
+    to_y = jnp.logical_or(host_wants(y_row), host_wants(diagonal))
     y_of_owner = row == (owner_row + half_z) % n_row
     is_relay = jnp.logical_and(y_of_owner, wants_column(x_row))
 
@@ -144,12 +155,12 @@
 
     for step in range(1, n_row):
         hello(barrier, (row + step) % n_row, col)
+        hello(barrier, (row + step) % n_row, partner)
     hello(barrier, row, partner)
     for chip in range(1, n_z):
         @pl.when(z < chip)
         def _(chip=chip):
-            hello(barrier, row, 2 * chip)
-            hello(barrier, row, 2 * chip + 1)
+            hello(barrier, row, 2 * chip + core)
 
     loads = [
         pltpu.make_async_copy(locs, loc_all.at[col, pl.ds(0, slots)], load_sem.at[0]),
@@ -193,7 +204,7 @@
     def chunk(step):
         block = 2 * chip_at(step // 2) + (core + step) % 2
 
-        @pl.when(step > 0)
+        @pl.when(step % 2 == 1)
         def _():
             loc_copy(block, partner).wait_recv()
 
@@ -260,20 +271,18 @@
     @pl.when(corner == 1)
     def _():
         own_all()
-    pl.semaphore_wait(barrier, n_row + 2 * z)
+    pl.semaphore_wait(barrier, 2 * n_row - 1 + z)
 
     for chip in range(n_z - 1):
         @pl.when(z > chip)
         def _(chip=chip):
-            hello(far_sem, row, 2 * chip)
-            hello(far_sem, row, 2 * chip + 1)
+            hello(far_sem, row, 2 * chip + core)
 
     def each_loc(act, higher):
         for chip in range(n_z):
             @pl.when(z < chip if higher else z > chip)
             def _(chip=chip):
-                act(loc_copy(col, 2 * chip))
-                act(loc_copy(col, 2 * chip + 1))
+                act(loc_copy(col, 2 * chip + core))
 
     def each_direct(act, higher, slot):
         for chip in (range(1, n_z) if higher else reversed(range(n_z - 1))):
@@ -290,24 +299,22 @@
                 act(pv_copy(slot, row, target))
 
     def straight(step):
-        if step == n_z - 1:
-            return True
-        return False
+        return step >= n_z - 2
 
     def each_column(act, block, step, slot=None):
-        ours = is_owner if slot is None else jnp.logical_and(is_owner, owner_slot == slot)
+        ours = is_host if slot is None else jnp.logical_and(is_host, host_slot == slot)
         far = straight(step)
 
-        @when(ours, wants_column(x_row))
+        @when(ours, host_wants(x_row))
         def _():
             act(pj_copy(block, 0))
 
-        @when(ours, wants_column(y_row) if far is True else to_y)
+        @when(ours, host_wants(y_row) if far is True else to_y)
         def _():
             act(pj_copy(block, 1))
 
         if far is not False:
-            @when(ours, wants_column(diagonal), far)
+            @when(ours, host_wants(diagonal), far)
             def _():
                 act(pj_copy(block, 3))
 
@@ -350,19 +357,8 @@
             pu_partner(slot, block).start()
             each_column(start, block, step, slot)
 
-    def spreads(slot):
-        return jnp.logical_and(is_owner, owner_slot == slot)
-
-    def from_partner(slot, step):
-        block = 2 * chip_at(step) + other
-
-        @when(needs(slot, z), spreads(slot))
-        def _():
-            pu_partner(slot, block).wait_recv()
-            each_column(start, block, step, slot)
-
     def settle_rows(slot, first, final):
-        @when(needs(slot, z), jnp.logical_not(spreads(slot)))
+        @pl.when(needs(slot, z))
         def _():
             for step in range(first, final):
                 pu_partner(slot, 2 * chip_at(step) + other).wait_recv()
@@ -377,13 +373,11 @@
             for block in pair(step):
                 pj_copy(block, 0).wait_recv()
 
-                @pl.when(jnp.logical_not(straight(step)))
-                def _(block=block):
-                    pj_copy(block, 2).start()
+                pj_copy(block, 2).start()
 
     def settle_column(first, final):
         for step in range(first, final):
-            late = step == n_z - 1
+            late = straight(step)
 
             @when(jnp.logical_not(is_owner), wants_column(row),
                   True if late else jnp.logical_not(is_relay))
@@ -463,11 +457,16 @@
     def upward():
         @pl.when(z < n_z - 1)
         def _():
-            pl.semaphore_wait(far_sem, 2 * (n_z - 1 - z))
+            pl.semaphore_wait(far_sem, n_z - 1 - z)
         each_loc(start, True)
         for slot in range(slots):
             each_direct(start, True, slot)
 
+    def points_of(step):
+        block = 2 * chip_at(step) + core
+        loc_copy(block, partner).wait_recv()
+        loc_forward(block).start()
+
     def early(slot, step):
         @pl.when(jnp.logical_or(z > 0, hosts(slot)))
         def _():
@@ -503,10 +502,8 @@
     def _():
         for slot in range(1, slots):
             send_lower(slot)
-    from_partner(0, 0)
+    points_of(1)
     chunks(2, 3)
-    for slot in range(1, slots):
-        from_partner(slot, 0)
     @pl.when(z > 0)
     def _():
         arrive(0, 1)
@@ -516,37 +513,35 @@
     def _():
         arrive(0, 2)
     gram_swap(0)
+    points_of(2)
     chunks(3, 4)
 
     @pl.when(z == 0)
     def _():
         arrive(0, 1)
     gram_sum(0)
-    from_partner(0, 1)
     for slot in range(1, slots):
         early(slot, 1)
 
     @when(z == 0, hosts(0))
     def _():
         arrive(0, 2)
+    chunks(4, 5)
+    for slot in range(1, slots):
+        early(slot, 2)
     each_gram(start, 0)
-    chunks(4, 5)
-    for slot in range(1, slots):
-        early(slot, 2)
-        from_partner(slot, 1)
+    for slot in range(1, slots):
         gram_part(slot)
-    from_partner(0, 2)
     column(0)
     for slot in range(1, slots):
         gram_swap(slot)
     early(0, 3)
+    points_of(3)
     chunks(5, 6)
     for slot in range(1, slots):
         gram_sum(slot)
         late(slot, 1)
-        from_partner(slot, 2)
     late(0, 2)
-    from_partner(0, 3)
     for slot in range(1, slots):
         each_gram(start, slot)
     chunks(6, 7)
@@ -557,17 +552,26 @@
     for slot in range(1, slots):
         settle_rows(slot, 0, n_z - 2)
     late(0, 3)
-    column(2)
     for slot in range(1, slots):
         late(slot, 2)
     settle_rows(0, 0, n_z)
     pend_acc[...] = acc[...] * matern_scale
+    at_diagonal = row == n_row - 1 - owner_row
+
+    @pl.when(jnp.logical_not(at_diagonal))
+    def _():
+        settle_column(0, n_z - 1)
+    for slot in range(1, slots):
+        late(slot, 3)
+        settle_rows(slot, n_z - 2, n_z - 1)
 
     wait_send(loc_copy(col, partner))
     for higher in (False, True):
         each_loc(wait_send, higher)
         for slot in range(slots):
             each_direct(wait_send, higher, slot)
+    for step in range(1, n_z):
+        loc_forward(2 * chip_at(step) + core).wait_send()
 
     def forwards_done(slot, first, final):
         for step in range(first, final):
@@ -582,10 +586,9 @@
                 pu_relay(slot, block).wait_send()
 
     def columns_done(step):
-        for block in pair(step):
-            each_column(wait_send, block, step)
-        if step < n_z - 1:
-            @when(is_relay, jnp.logical_not(straight(step)))
+        each_column(wait_send, 2 * chip_at(step) + core, step)
+        if not straight(step):
+            @pl.when(is_relay)
             def _():
                 for block in pair(step):
                     pj_copy(block, 2).wait_send()
@@ -596,18 +599,27 @@
         @pl.when(has_batch(slot))
         def _(slot=slot):
             gx_copy(slot).wait_send()
-        each_gram(wait_send, slot)
-        forwards_done(slot, 0, n_z - 1)
-    forwards_done(0, n_z - 1, n_z)
-    for step in range(n_z - 1):
-        columns_done(step)
-    for slot in range(1, slots):
-        late(slot, 3)
-        from_partner(slot, 3)
-    settle_column(0, n_z - 1)
-    for slot in range(1, slots):
-        settle_rows(slot, n_z - 2, n_z)
+
+    @pl.when(at_diagonal)
+    def _():
+        settle_column(0, n_z - 1)
     settle_column(n_z - 1, n_z)
+
+    nothing = jnp.zeros((rank_dim, 2 * rank_dim), jnp.bfloat16)
+
+    def stacked(value):
+        high, low = halves(value)
+        return jnp.concatenate([
+            jnp.concatenate([high, high], axis=1), jnp.concatenate([low, nothing], axis=1)
+        ], axis=0)
+
+    def right_of(slot):
+        @pl.when(active(slot))
+        def _():
+            lanes = slice(slot * rank_dim, (slot + 1) * rank_dim)
+            right_core = dot3(row_sketch[slot], gram_all[:, lanes], NT)
+            z_left[slot] = stacked(
+                jnp.concatenate([own_sketches[slot, 1], -right_core], axis=1))
 
     @pl.when(any_active)
     def _():
@@ -616,29 +628,27 @@
             chip = chip_at(step)
             g_copy(chip, z).wait_recv()
             gram = gram + g_all[chip]
+        gram_all[...] = gram
         left_core = dot3(col_sketch[...], gram, NN)
-        nothing = jnp.zeros((rank_dim, 2 * rank_dim), jnp.bfloat16)
-
-        def stacked(value):
-            high, low = halves(value)
-            return jnp.concatenate([
-                jnp.concatenate([high, high], axis=1), jnp.concatenate([low, nothing], axis=1)
-            ], axis=0)
-
         for slot in range(slots):
             lanes = slice(slot * rank_dim, (slot + 1) * rank_dim)
 
             @pl.when(active(slot))
             def _(slot=slot, lanes=lanes):
-                right_core = dot3(row_sketch[slot], gram[:, lanes], NT)
                 y_left[slot] = stacked(
                     jnp.concatenate([own_sketches[slot, 0], -left_core[:, lanes]], axis=1))
-                z_left[slot] = stacked(
-                    jnp.concatenate([own_sketches[slot, 1], -right_core], axis=1))
-
+    right_of(0)
+    for slot in range(slots):
+        each_gram(wait_send, slot)
+        forwards_done(slot, 0, n_z - 1)
+    forwards_done(0, n_z - 1, n_z)
+    for step in range(n_z):
+        columns_done(step)
+    for slot in range(1, slots):
+        settle_rows(slot, n_z - 1, n_z)
+        right_of(slot)
     for slot in range(1, slots):
         forwards_done(slot, n_z - 1, n_z)
-    columns_done(n_z - 1)
 
 
 def finish(
@@ -837,8 +847,9 @@
             pltpu.VMEM((slots, 2, rank_dim, rank_dim), f32),
             pltpu.VMEM((slots, rank_dim, rank_dim), f32),
             pltpu.VMEM((rank_dim, rank_dim), f32),
+            pltpu.VMEM((rank_dim, flat), f32),
             pltpu.SemaphoreType.REGULAR,
-            dma((6,)), dma((slots, 2)), dma((n_col,)), dma((n_col,)),
+            dma((6,)), dma((slots, 2)), dma((n_col,)), dma((n_col,)), dma((n_col,)),
             dma((slots, n_z)), dma((slots, n_col)), dma((slots, n_col)), dma((slots, n_col)),
             dma((slots, n_row)), dma((slots, n_row)),
             dma((4, n_col)), dma((n_col,)),

time: 24.6 us -> 23.8 us (0.967)
  Pallas kernels: 23.6 us -> 23 us
    pallas_call x1, Pallas kernels: 21.9 us -> 21.2 us  [on_device(): pl.pallas_call(functools.partial(kernel, n_row, n_col), out_shape=(pltpu....]
where the time goes in v5:
time: 23.8 us; the launch traced here: 23.6 us
  Pallas kernels  23 us (97%)
  between operations  0.64 us (3%)
    pallas_call x1, Pallas kernels, on_device(): pl.pallas_call(functools.partial(kernel, n_row, n_col), out_shape=(pltpu....  21.2 us
    pallas_call x1, Pallas kernels, on_device(): pl.pallas_call(functools.partial(finish, n_row), out_shape=(shape((slots,...  1.79 us

profile of v5, /device:TPU:6, one launch (start us, length us, event | category | flops | bytes accessed | tf_op | source)
XLA Modules:
  0.0 23.6 jit_solution(10004918956678500637)
XLA Ops:
  0.6 21.2 %shard_map.111 = (bf16[2,2,64,2048]{3,2,1,0:T(8,128)(2,1)S(1)}, bf16[2,2,64,2048]{3,2,1,0:T(8,128)(2,1)S(1)}, bf16[2,2,64,2048]{3,2,1,0:T(8,128)(2,1)S(1)}, bf16...) custom-call(s32[2]{0:T(128)} %bitcast.11, ...), custom_call_target="tpu_custom_call" | custom-call | tf_op jit(solution)/shard_map/pallas_call | solution.py:815
  21.8 1.8 %shard_map.112 = (f32[2,1,1,64,2048]{4,3,2,1,0:T(8,128)}, f32[2,1,1,64,2048]{4,3,2,1,0:T(8,128)}, f32[2,1,64,256]{3,2,1,0:T(8,128)}, f32[2,1,64,256]{3,2,1,0:T(8,128)}) custom-call(bf16[2,2,64,2048]{3,2,1,0:T(8,128)(2,1)S(1)} %get-tuple-element.11.ru, bf16[2,2,64,2048]{3,2,1,0:T(8,128)(2,1)S(1)} %get-tuple-element.12.rv, ...), custom_call_target="tpu_custom_call" | custom-call | tf_op jit(solution)/shard_map/pallas_call | solution.py:874

commit v6 on v5

--- a/solution.py
+++ b/solution.py
@@ -50,7 +50,7 @@
     ru, rv, rp, rj, y_left, z_left, pend_acc,
     ranks, u_buf, v_buf, sk_buf, loc_all, pu_all, pj_all, pv_all, g_part, g_peer, g_sum, g_all,
     points, own_points, sk_both, mat_high, mat_low, acc, own_sketches, row_sketch, col_sketch, gram_all,
-    far_sem, load_sem, trail_sem, loc_send, lf_send, loc_recv, pu_send, pf_send, pr_send, pu_recv,
+    far_sem, load_sem, loc_send, lf_send, loc_recv, pu_send, pf_send, pu_recv,
     pv_send, pv_recv, pj_send, pj_recv, gx_send, gx_recv, g_send, g_recv,
 ):
     row, col = lax.axis_index("row"), lax.axis_index("col")
@@ -100,11 +100,11 @@
             device_id=(to_row, to_col), device_id_type=MESH)
 
     def loc_copy(source, target):
-        return remote(loc_all.at[source], loc_all.at[source], loc_send.at[target],
+        return remote(loc_all.at[source], loc_all.at[source], loc_send.at[target // 2],
                       loc_recv.at[source], row, target)
 
     def loc_forward(block):
-        return remote(loc_all.at[block], loc_all.at[block], lf_send.at[block],
+        return remote(loc_all.at[block], loc_all.at[block], lf_send,
                       loc_recv.at[block], row, partner)
 
     def pv_copy(slot, source, target):
@@ -119,14 +119,15 @@
         return pu_copy(slot, col, pu_send.at[slot, chip], 2 * chip + core)
 
     def pu_partner(slot, block):
-        return pu_copy(slot, block, pf_send.at[slot, block], partner)
+        return pu_copy(slot, block, pf_send.at[slot], partner)
 
     def pu_relay(slot, block):
-        return pu_copy(slot, block, pr_send.at[slot, block], core)
+        return pu_copy(slot, block, pu_send.at[slot, n_z + block // 2 - 2], core)
 
     def pj_copy(block, way):
         src = pj_all.at[block] if way == 2 else pu_all.at[block, host_slot]
-        return remote(src, pj_all.at[block], pj_send.at[way, block], pj_recv.at[block],
+        return remote(src, pj_all.at[block], pj_send.at[block % 2, block // 2] if way == 2 else pj_send.at[way % 3 + way // 3 * 2, block // 2],
+                      pj_recv.at[block],
                       (x_row, y_row, x_row, diagonal)[way], col if way == 2 else host_col)
 
     def gx_copy(batch):
@@ -175,30 +176,34 @@
 
     def trail_load(slot, which):
         src, dst = ((trail_u, u_buf), (trail_v, v_buf))[which]
-        return pltpu.make_async_copy(src.at[slot], dst.at[slot], trail_sem.at[slot, which])
-
+        return pltpu.make_async_copy(src.at[slot], dst.at[slot], load_sem.at[2 * slot + which])
+
+    for load in loads[:4]:
+        load.wait()
     for slot in range(slots):
         @pl.when(active(slot))
         def _(slot=slot):
             trail_load(slot, 0).start()
             trail_load(slot, 1).start()
 
-    for load in loads:
-        load.wait()
-    sk_high, sk_low = halves(sk_buf[...])
-    for block in range(n_col):
-        sk_both[block, 0:rank_dim] = sk_high[:, block * w:(block + 1) * w]
-        sk_both[block, rank_dim:2 * rank_dim] = sk_low[:, block * w:(block + 1) * w]
-
-    acc[...] = jnp.zeros_like(acc)
-    row_sketch[...] = jnp.zeros_like(row_sketch)
-    col_sketch[...] = jnp.zeros_like(col_sketch)
-    own_points[0:1, :] = jnp.concatenate(
-        [loc_all[col, slot, 0:1] for slot in range(slots)] + [loc_all[col, slots, 0:1]] * slots,
-        axis=1) * point_scale
-    own_points[1:2, :] = jnp.concatenate(
-        [loc_all[col, slot, 1:2] for slot in range(slots)] + [loc_all[col, slots, 1:2]] * slots,
-        axis=1) * point_scale
+    def prepare():
+        for load in loads[4:]:
+            load.wait()
+        sk_high, sk_low = halves(sk_buf[...])
+        for block in range(n_col):
+            sk_both[block, 0:rank_dim] = sk_high[:, block * w:(block + 1) * w]
+            sk_both[block, rank_dim:2 * rank_dim] = sk_low[:, block * w:(block + 1) * w]
+
+        acc[...] = jnp.zeros_like(acc)
+        row_sketch[...] = jnp.zeros_like(row_sketch)
+        col_sketch[...] = jnp.zeros_like(col_sketch)
+        own_points[0:1, :] = jnp.concatenate(
+            [loc_all[col, slot, 0:1] for slot in range(slots)] + [loc_all[col, slots, 0:1]] * slots,
+            axis=1) * point_scale
+        own_points[1:2, :] = jnp.concatenate(
+            [loc_all[col, slot, 1:2] for slot in range(slots)] + [loc_all[col, slots, 1:2]] * slots,
+            axis=1) * point_scale
+
     pad_rows = points.shape[2] - 2 * slots - 2
 
     def chunk(step):
@@ -266,10 +271,11 @@
                 own_sketch(slot)
 
     corner = (n_row - row) // n_row
-    pl.loop(0, corner)(chunk)
 
     @pl.when(corner == 1)
     def _():
+        prepare()
+        chunk(0)
         own_all()
     pl.semaphore_wait(barrier, 2 * n_row - 1 + z)
 
@@ -354,6 +360,7 @@
             @when(z == 1, chip >= 2)
             def _():
                 pu_relay(slot, block).start()
+            pu_partner(slot, col).wait_send()
             pu_partner(slot, block).start()
             each_column(start, block, step, slot)
 
@@ -465,6 +472,8 @@
     def points_of(step):
         block = 2 * chip_at(step) + core
         loc_copy(block, partner).wait_recv()
+        if step > 1:
+            loc_forward(block).wait_send()
         loc_forward(block).start()
 
     def early(slot, step):
@@ -478,7 +487,11 @@
             arrive(slot, step)
 
     top = n_z - 1
-    pl.loop(corner, 1)(chunk)
+
+    @pl.when(corner == 0)
+    def _():
+        prepare()
+        chunk(0)
 
     @pl.when(z == top)
     def _():
@@ -547,11 +560,11 @@
     chunks(6, 7)
     for slot in range(1, slots):
         early(slot, 3)
+    late(0, 3)
+    chunks(7, 8)
+    for slot in range(1, slots):
+        settle_rows(slot, 0, n_z - 2)
     column(1)
-    chunks(7, 8)
-    for slot in range(1, slots):
-        settle_rows(slot, 0, n_z - 2)
-    late(0, 3)
     for slot in range(1, slots):
         late(slot, 2)
     settle_rows(0, 0, n_z)
@@ -560,7 +573,7 @@
 
     @pl.when(jnp.logical_not(at_diagonal))
     def _():
-        settle_column(0, n_z - 1)
+        settle_column(0, n_z - 2)
     for slot in range(1, slots):
         late(slot, 3)
         settle_rows(slot, n_z - 2, n_z - 1)
@@ -570,20 +583,20 @@
         each_loc(wait_send, higher)
         for slot in range(slots):
             each_direct(wait_send, higher, slot)
-    for step in range(1, n_z):
-        loc_forward(2 * chip_at(step) + core).wait_send()
-
-    def forwards_done(slot, first, final):
-        for step in range(first, final):
+    loc_forward(col).wait_send()
+
+    def relays_done(slot):
+        for step in range(1, n_z):
             block = 2 * chip_at(step) + core
-
-            @pl.when(needs(slot, z))
-            def _(block=block):
-                pu_partner(slot, block).wait_send()
 
             @when(z == 1, chip_at(step) >= 2, needs(slot, z))
             def _(block=block):
                 pu_relay(slot, block).wait_send()
+
+    def forwards_done(slot):
+        @pl.when(needs(slot, z))
+        def _():
+            pu_partner(slot, col).wait_send()
 
     def columns_done(step):
         each_column(wait_send, 2 * chip_at(step) + core, step)
@@ -602,8 +615,8 @@
 
     @pl.when(at_diagonal)
     def _():
-        settle_column(0, n_z - 1)
-    settle_column(n_z - 1, n_z)
+        settle_column(0, n_z - 2)
+    settle_column(n_z - 2, n_z)
 
     nothing = jnp.zeros((rank_dim, 2 * rank_dim), jnp.bfloat16)
 
@@ -640,15 +653,14 @@
     right_of(0)
     for slot in range(slots):
         each_gram(wait_send, slot)
-        forwards_done(slot, 0, n_z - 1)
-    forwards_done(0, n_z - 1, n_z)
+        relays_done(slot)
+    forwards_done(0)
     for step in range(n_z):
         columns_done(step)
     for slot in range(1, slots):
+        forwards_done(slot)
         settle_rows(slot, n_z - 1, n_z)
         right_of(slot)
-    for slot in range(1, slots):
-        forwards_done(slot, n_z - 1, n_z)
 
 
 def finish(
@@ -849,10 +861,10 @@
             pltpu.VMEM((rank_dim, rank_dim), f32),
             pltpu.VMEM((rank_dim, flat), f32),
             pltpu.SemaphoreType.REGULAR,
-            dma((6,)), dma((slots, 2)), dma((n_col,)), dma((n_col,)), dma((n_col,)),
-            dma((slots, n_z)), dma((slots, n_col)), dma((slots, n_col)), dma((slots, n_col)),
+            dma((6,)), dma((n_z,)), dma, dma((n_col,)),
+            dma((slots, 2 * n_z - 2)), dma((slots,)), dma((slots, n_col)),
             dma((slots, n_row)), dma((slots, n_row)),
-            dma((4, n_col)), dma((n_col,)),
+            dma((3, n_z)), dma((n_col,)),
             dma((slots,)), dma((slots,)), dma((n_z,)), dma((n_z,)),
         ],
         compiler_params=pltpu.CompilerParams(
@@ -870,7 +882,7 @@
         )
     ])
     kept = [pltpu.with_memory_space_constraint(value, pltpu.VMEM) for value in kept]
-    pieces = 2
+    pieces = 4
     return pl.pallas_call(
         functools.partial(finish, n_row),
         out_shape=(

time: 23.8 us -> 23.4 us (0.983)
  the two profiles are of different devices: /device:TPU:6 before, /device:TPU:0 now
where the time goes in v6:
time: 23.4 us; the launch traced here: 23.2 us
  Pallas kernels  22.6 us (97%)
  between operations  0.64 us (3%)
    pallas_call x1, Pallas kernels, on_device(): pl.pallas_call(functools.partial(kernel, n_row, n_col), out_shape=(pltpu....  21 us
    pallas_call x1, Pallas kernels, on_device(): pl.pallas_call(functools.partial(finish, n_row), out_shape=(shape((slots,...  1.56 us

profile of v6, /device:TPU:0, one launch (start us, length us, event | category | flops | bytes accessed | tf_op | source)
XLA Modules:
  0.0 23.2 jit_solution(8279312697052216843)
XLA Ops:
  0.6 21.0 %shard_map.111 = (bf16[2,2,64,2048]{3,2,1,0:T(8,128)(2,1)S(1)}, bf16[2,2,64,2048]{3,2,1,0:T(8,128)(2,1)S(1)}, bf16[2,2,64,2048]{3,2,1,0:T(8,128)(2,1)S(1)}, bf16...) custom-call(s32[2]{0:T(128)} %bitcast.11, ...), custom_call_target="tpu_custom_call" | custom-call | tf_op jit(solution)/shard_map/pallas_call | solution.py:827
  21.7 1.6 %shard_map.112 = (f32[2,1,1,64,2048]{4,3,2,1,0:T(8,128)}, f32[2,1,1,64,2048]{4,3,2,1,0:T(8,128)}, f32[2,1,64,256]{3,2,1,0:T(8,128)}, f32[2,1,64,256]{3,2,1,0:T(8,128)}) custom-call(bf16[2,2,64,2048]{3,2,1,0:T(8,128)(2,1)S(1)} %get-tuple-element.11.ru, bf16[2,2,64,2048]{3,2,1,0:T(8,128)(2,1)S(1)} %get-tuple-element.12.rv, ...), custom_call_target="tpu_custom_call" | custom-call | tf_op jit(solution)/shard_map/pallas_call | solution.py:886

commit v7 on v6

--- a/solution.py
+++ b/solution.py
@@ -882,7 +882,7 @@
         )
     ])
     kept = [pltpu.with_memory_space_constraint(value, pltpu.VMEM) for value in kept]
-    pieces = 4
+    pieces = 2
     return pl.pallas_call(
         functools.partial(finish, n_row),
         out_shape=(

time: 23.4 us -> 23.4 us (level)
  no operation moved by 1% of the time
where the time goes in v7:
time: 23.4 us; the launch traced here: 23.2 us
  Pallas kernels  22.5 us (96%)
  between operations  0.64 us (3%)
    pallas_call x1, Pallas kernels, on_device(): pl.pallas_call(functools.partial(kernel, n_row, n_col), out_shape=(pltpu....  21 us
    pallas_call x1, Pallas kernels, on_device(): pl.pallas_call(functools.partial(finish, n_row), out_shape=(shape((slots,...  1.5 us

profile of v7, /device:TPU:0, one launch (start us, length us, event | category | flops | bytes accessed | tf_op | source)
XLA Modules:
  0.0 23.2 jit_solution(17477488574218702548)
XLA Ops:
  0.6 21.0 %shard_map.111 = (bf16[2,2,64,2048]{3,2,1,0:T(8,128)(2,1)S(1)}, bf16[2,2,64,2048]{3,2,1,0:T(8,128)(2,1)S(1)}, bf16[2,2,64,2048]{3,2,1,0:T(8,128)(2,1)S(1)}, bf16...) custom-call(s32[2]{0:T(128)} %bitcast.11, ...), custom_call_target="tpu_custom_call" | custom-call | tf_op jit(solution)/shard_map/pallas_call | solution.py:827
  21.7 1.5 %shard_map.112 = (f32[2,1,1,64,2048]{4,3,2,1,0:T(8,128)}, f32[2,1,1,64,2048]{4,3,2,1,0:T(8,128)}, f32[2,1,64,256]{3,2,1,0:T(8,128)}, f32[2,1,64,256]{3,2,1,0:T(8,128)}) custom-call(bf16[2,2,64,2048]{3,2,1,0:T(8,128)(2,1)S(1)} %get-tuple-element.11.ru, bf16[2,2,64,2048]{3,2,1,0:T(8,128)(2,1)S(1)} %get-tuple-element.12.rv, ...), custom_call_target="tpu_custom_call" | custom-call | tf_op jit(solution)/shard_map/pallas_call | solution.py:886
